TPU v7x, 32 devices: a 4x4x1 block of a 4x4x8 slice. The times are simulated.
32 devices in a mesh: data: 1 (over z), time: 32 (over y, x, core).
Axes of the slice: x: 4, y: 4, z: 1, core: 2. Of those that a mesh axis runs over, the one named last changes fastest.
The devices are a block of a 4x4x8 slice.
Arguments:
- x_init: float32 [64, 256, 16], P('data')
- w_in: bfloat16 [16, 384], replicated
- w_out: bfloat16 [384, 16], replicated
- mod_scale: bfloat16 [64, 384], P('time')
- mod_shift: bfloat16 [64, 384], P('time')
- step_size: float32 [64], P('time')
Outputs:
- output: float32 [64, 64, 256, 16], P('time', 'data')
All inputs are finite; a program needn't handle non-finite values.
Results may differ from a plain program's by a relative error of at most 0.001.
Values are sent between devices in bfloat16 or wider.
A program may use at most 768 MiB of HBM per device.

v0:
```python
import jax
import jax.numpy as jnp
from jax import lax
from jax.sharding import PartitionSpec as P

SWEEPS = 4


def drift_block(pre_act, scale, shift, w_out):
    hidden_act = jax.nn.gelu(pre_act * scale + shift, approximate=True)
    return jnp.einsum("kbnd,dc->kbnc", hidden_act.astype(jnp.bfloat16), w_out, preferred_element_type=jnp.float32)


def solution(mesh):
    n_time = mesh.shape["time"]
    from_next = [(source, source - 1) for source in range(1, n_time)]
    hop_dists = [2 ** power for power in range(n_time) if 2 ** power < n_time]

    def local(x_init, w_in, w_out, mod_scale, mod_shift, step_size):
        scale = (1.0 + mod_scale.astype(jnp.float32))[:, None, None, :]
        shift = mod_shift.astype(jnp.float32)[:, None, None, :]
        pre_act = jnp.einsum("bnc,cd->bnd", x_init.astype(jnp.bfloat16), w_in, preferred_element_type=jnp.float32)[None]
        latents = None
        for sweep in range(SWEEPS):
            if sweep > 0:
                pre_act = jnp.einsum("kbnc,cd->kbnd", latents.astype(jnp.bfloat16), w_in, preferred_element_type=jnp.float32)
            drifts = drift_block(pre_act, scale, shift, w_out)
            next_first = lax.ppermute(drifts[0], "time", from_next)
            next_drifts = jnp.concatenate([drifts[1:], next_first[None]], axis=0)
            increments = step_size[:, None, None, None] * (0.5 * (drifts + next_drifts))
            local_cum = jnp.cumsum(increments, axis=0)
            local_excl = jnp.concatenate([jnp.zeros_like(local_cum[:1]), local_cum[:-1]], axis=0)
            dev_total = local_cum[-1]
            inclusive = dev_total
            for distance in hop_dists:
                inclusive = inclusive + lax.ppermute(inclusive, "time", [(source, source + distance) for source in range(n_time - distance)])
            offset = inclusive - dev_total
            latents = x_init[None] + (offset[None] + local_excl)
        return latents

    return jax.shard_map(local, mesh=mesh, in_specs=(P("data"), P(), P(), P("time"), P("time"), P("time")), out_specs=P("time", "data"), check_vma=False)
```

profile of v0, /device:TPU:102, one launch (start us, length us, event | category | flops | bytes accessed | tf_op | source)
XLA Modules:
  0.0 659.7 jit_solution(18091580024323217654)
XLA Ops:
  1.4 4.7 fusion.82
  6.1 19.2 %fusion.32 = f32[2,64,256,16]{2,3,1,0:T(8,128)S(1)} fusion(f32[2,384]{1,0:T(2,128)S(1)} %convert_element_type.32, f32[2,384]{1,0:T(2,128)S(1)} %convert_add_fusion, f32[64,256,384]{2,1,0:T(8,128)S(1)} %fusion.82, bf16[384,16]{0,1:T(8,128)(2,1)S(1)} %copy-done.2), kind=kOutput, calls=%fused_computation.36 | convolution fusion | flops 541065216 | bytes 27281408 | tf_op jit(solution)/shard_map/kbnd,dc->kbnc/dot_general | solution.py:11
  27.6 12.3 %collective-permute-done = f32[64,256,16]{1,2,0:T(8,128)S(1)} collective-permute-done((f32[64,256,16]{1,2,0:T(8,128)S(1)}, f32[64,256,16]{1,2,0:T(8,128)S(1)}, u32[]{:S(2)}, u32[]{:S(2)}) %collective-permute-start) | collective-permute-done | bytes 1048608 | tf_op jit(solution)/shard_map/ppermute | solution.py:28
  41.7 5.7 collective-permute-start.1
  47.3 10.7 %collective-permute-done.1 = f32[64,256,16]{1,2,0:T(8,128)S(1)} collective-permute-done((f32[64,256,16]{1,2,0:T(8,128)S(1)}, f32[64,256,16]{1,2,0:T(8,128)S(1)}, u32[]{:S(2)}, u32[]{:S(2)}) %collective-permute-start.1) | collective-permute-done | bytes 1048608 | tf_op jit(solution)/shard_map/ppermute | solution.py:36
  58.2 7.5 %collective-permute-start.2 = (f32[64,256,16]{1,2,0:T(8,128)S(1)}, f32[64,256,16]{1,2,0:T(8,128)S(1)}, u32[]{:S(2)}, u32[]{:S(2)}) collective-permute-start(f32[64,256,16]{1,2,0:T(8,128)S(1)} %fusion.121), channel_id=1, source_target_pairs={{0,2},{1,3},{2,4},{3,5},{4,6},{5,7},{6,8},{7,9},{8,10},{9,11},{10,... | collective-permute-start | bytes 3145736 | tf_op jit(solution)/shard_map/ppermute | solution.py:36
  65.7 20.4 %collective-permute-done.2 = f32[64,256,16]{1,2,0:T(8,128)S(1)} collective-permute-done((f32[64,256,16]{1,2,0:T(8,128)S(1)}, f32[64,256,16]{1,2,0:T(8,128)S(1)}, u32[]{:S(2)}, u32[]{:S(2)}) %collective-permute-start.2) | collective-permute-done | bytes 1048608 | tf_op jit(solution)/shard_map/ppermute | solution.py:36
  86.3 2.8 collective-permute-start.3
  89.1 26.0 %collective-permute-done.3 = f32[64,256,16]{1,2,0:T(8,128)S(1)} collective-permute-done((f32[64,256,16]{1,2,0:T(8,128)S(1)}, f32[64,256,16]{1,2,0:T(8,128)S(1)}, u32[]{:S(2)}, u32[]{:S(2)}) %collective-permute-start.3) | collective-permute-done | bytes 1048608 | tf_op jit(solution)/shard_map/ppermute | solution.py:36
  115.3 4.1 collective-permute-start.4
  119.5 21.5 %collective-permute-done.4 = f32[64,256,16]{1,2,0:T(8,128)S(1)} collective-permute-done((f32[64,256,16]{1,2,0:T(8,128)S(1)}, f32[64,256,16]{1,2,0:T(8,128)S(1)}, u32[]{:S(2)}, u32[]{:S(2)}) %collective-permute-start.4) | collective-permute-done | bytes 1048608 | tf_op jit(solution)/shard_map/ppermute | solution.py:36
  141.2 7.1 %collective-permute-start.5 = (f32[64,256,16]{1,2,0:T(8,128)S(1)}, f32[64,256,16]{1,2,0:T(8,128)S(1)}, u32[]{:S(2)}, u32[]{:S(2)}) collective-permute-start(f32[64,256,16]{1,2,0:T(8,128)S(1)} %add.205), channel_id=1, source_target_pairs={{0,16},{1,17},{2,18},{3,19},{4,20},{5,21},{6,22},{7,23},{8,24},{9,... | collective-permute-start | bytes 3145736 | tf_op jit(solution)/shard_map/ppermute | solution.py:36
  148.3 20.6 %collective-permute-done.5 = f32[64,256,16]{1,2,0:T(8,128)S(1)} collective-permute-done((f32[64,256,16]{1,2,0:T(8,128)S(1)}, f32[64,256,16]{1,2,0:T(8,128)S(1)}, u32[]{:S(2)}, u32[]{:S(2)}) %collective-permute-start.5) | collective-permute-done | bytes 1048608 | tf_op jit(solution)/shard_map/ppermute | solution.py:36
  170.3 22.0 %fusion.38 = f32[2,64,256,16]{2,3,1,0:T(8,128)S(1)} fusion(f32[2,384]{1,0:T(2,128)S(1)} %convert_element_type.32, f32[2,384]{1,0:T(2,128)S(1)} %convert_add_fusion, f32[1,64,256,16]{2,3,1,0:T(8,128)} %get-tuple-element.18, f32[64,256,16]{1,2,0:T(8,128)} %add_subtract_fusion.3, f32[64,256,16]{1,2,0:T(8,128)S(1)} %copy-done.1, ...), kind=kOutput, calls=%fused_computation.39 | convolution fusion | flops 945291264 | bytes 5273600 | tf_op jit(solution)/shard_map/kbnd,dc->kbnc/dot_general | solution.py:11
  192.5 12.0 %collective-permute-start.6 = (f32[64,256,16]{1,2,0:T(8,128)S(1)}, f32[64,256,16]{1,2,0:T(8,128)S(1)}, u32[]{:S(2)}, u32[]{:S(2)}) collective-permute-start(f32[64,256,16]{1,2,0:T(8,128)S(1)} %get-tuple-element.16), channel_id=1, source_target_pairs={{1,0},{2,1},{3,2},{4,3},{5,4},{6,5},{7,6},{8,7},{9,8},{10,9},{11,1... | collective-permute-start | bytes 3145736 | tf_op jit(solution)/shard_map/ppermute | solution.py:28
  208.5 3.0 collective-permute-start.7
  211.6 13.3 %collective-permute-done.7 = f32[64,256,16]{1,2,0:T(8,128)S(1)} collective-permute-done((f32[64,256,16]{1,2,0:T(8,128)S(1)}, f32[64,256,16]{1,2,0:T(8,128)S(1)}, u32[]{:S(2)}, u32[]{:S(2)}) %collective-permute-start.7) | collective-permute-done | bytes 1048608 | tf_op jit(solution)/shard_map/ppermute | solution.py:36
  225.1 4.8 collective-permute-start.8
  229.9 20.5 %collective-permute-done.8 = f32[64,256,16]{1,2,0:T(8,128)S(1)} collective-permute-done((f32[64,256,16]{1,2,0:T(8,128)S(1)}, f32[64,256,16]{1,2,0:T(8,128)S(1)}, u32[]{:S(2)}, u32[]{:S(2)}) %collective-permute-start.8) | collective-permute-done | bytes 1048608 | tf_op jit(solution)/shard_map/ppermute | solution.py:36
  253.4 23.6 %collective-permute-done.9 = f32[64,256,16]{1,2,0:T(8,128)S(1)} collective-permute-done((f32[64,256,16]{1,2,0:T(8,128)S(1)}, f32[64,256,16]{1,2,0:T(8,128)S(1)}, u32[]{:S(2)}, u32[]{:S(2)}) %collective-permute-start.9) | collective-permute-done | bytes 1048608 | tf_op jit(solution)/shard_map/ppermute | solution.py:36
  277.2 4.5 collective-permute-start.10
  281.7 20.2 %collective-permute-done.10 = f32[64,256,16]{1,2,0:T(8,128)S(1)} collective-permute-done((f32[64,256,16]{1,2,0:T(8,128)S(1)}, f32[64,256,16]{1,2,0:T(8,128)S(1)}, u32[]{:S(2)}, u32[]{:S(2)}) %collective-permute-start.10) | collective-permute-done | bytes 1048608 | tf_op jit(solution)/shard_map/ppermute | solution.py:36
  302.0 4.8 collective-permute-start.11
  306.9 18.4 %collective-permute-done.11 = f32[64,256,16]{1,2,0:T(8,128)S(1)} collective-permute-done((f32[64,256,16]{1,2,0:T(8,128)S(1)}, f32[64,256,16]{1,2,0:T(8,128)S(1)}, u32[]{:S(2)}, u32[]{:S(2)}) %collective-permute-start.11) | collective-permute-done | bytes 1048608 | tf_op jit(solution)/shard_map/ppermute | solution.py:36
  326.7 22.0 %fusion.36 = f32[2,64,256,16]{2,3,1,0:T(8,128)S(1)} fusion(f32[2,384]{1,0:T(2,128)S(1)} %convert_element_type.32, f32[2,384]{1,0:T(2,128)S(1)} %convert_add_fusion, f32[1,64,256,16]{2,3,1,0:T(8,128)} %get-tuple-element.14, f32[64,256,16]{1,2,0:T(8,128)} %add_subtract_fusion.2, f32[64,256,16]{1,2,0:T(8,128)S(1)} %copy-done.1, ...), kind=kOutput, calls=%fused_computation.38 | convolution fusion | flops 945291264 | bytes 5273600 | tf_op jit(solution)/shard_map/kbnd,dc->kbnc/dot_general | solution.py:11
  351.1 12.1 %collective-permute-done.12 = f32[64,256,16]{1,2,0:T(8,128)S(1)} collective-permute-done((f32[64,256,16]{1,2,0:T(8,128)S(1)}, f32[64,256,16]{1,2,0:T(8,128)S(1)}, u32[]{:S(2)}, u32[]{:S(2)}) %collective-permute-start.12) | collective-permute-done | bytes 1048608 | tf_op jit(solution)/shard_map/ppermute | solution.py:28
  364.9 3.2 collective-permute-start.13
  368.1 13.2 %collective-permute-done.13 = f32[64,256,16]{1,2,0:T(8,128)S(1)} collective-permute-done((f32[64,256,16]{1,2,0:T(8,128)S(1)}, f32[64,256,16]{1,2,0:T(8,128)S(1)}, u32[]{:S(2)}, u32[]{:S(2)}) %collective-permute-start.13) | collective-permute-done | bytes 1048608 | tf_op jit(solution)/shard_map/ppermute | solution.py:36
  381.5 5.0 collective-permute-start.14
  386.5 23.5 %collective-permute-done.14 = f32[64,256,16]{1,2,0:T(8,128)S(1)} collective-permute-done((f32[64,256,16]{1,2,0:T(8,128)S(1)}, f32[64,256,16]{1,2,0:T(8,128)S(1)}, u32[]{:S(2)}, u32[]{:S(2)}) %collective-permute-start.14) | collective-permute-done | bytes 1048608 | tf_op jit(solution)/shard_map/ppermute | solution.py:36
  410.2 4.3 collective-permute-start.15
  414.5 24.4 %collective-permute-done.15 = f32[64,256,16]{1,2,0:T(8,128)S(1)} collective-permute-done((f32[64,256,16]{1,2,0:T(8,128)S(1)}, f32[64,256,16]{1,2,0:T(8,128)S(1)}, u32[]{:S(2)}, u32[]{:S(2)}) %collective-permute-start.15) | collective-permute-done | bytes 1048608 | tf_op jit(solution)/shard_map/ppermute | solution.py:36
  439.1 5.2 collective-permute-start.16
  444.2 20.3 %collective-permute-done.16 = f32[64,256,16]{1,2,0:T(8,128)S(1)} collective-permute-done((f32[64,256,16]{1,2,0:T(8,128)S(1)}, f32[64,256,16]{1,2,0:T(8,128)S(1)}, u32[]{:S(2)}, u32[]{:S(2)}) %collective-permute-start.16) | collective-permute-done | bytes 1048608 | tf_op jit(solution)/shard_map/ppermute | solution.py:36
  464.8 7.0 %collective-permute-start.17 = (f32[64,256,16]{1,2,0:T(8,128)S(1)}, f32[64,256,16]{1,2,0:T(8,128)S(1)}, u32[]{:S(2)}, u32[]{:S(2)}) collective-permute-start(f32[64,256,16]{1,2,0:T(8,128)S(1)} %add.229), channel_id=1, source_target_pairs={{0,16},{1,17},{2,18},{3,19},{4,20},{5,21},{6,22},{7,23},{8,24},{9,... | collective-permute-start | bytes 3145736 | tf_op jit(solution)/shard_map/ppermute | solution.py:36
  471.8 20.8 %collective-permute-done.17 = f32[64,256,16]{1,2,0:T(8,128)S(1)} collective-permute-done((f32[64,256,16]{1,2,0:T(8,128)S(1)}, f32[64,256,16]{1,2,0:T(8,128)S(1)}, u32[]{:S(2)}, u32[]{:S(2)}) %collective-permute-start.17) | collective-permute-done | bytes 1048608 | tf_op jit(solution)/shard_map/ppermute | solution.py:36
  493.9 22.0 %fusion.34 = f32[2,64,256,16]{2,3,1,0:T(8,128)S(1)} fusion(f32[2,384]{1,0:T(2,128)S(1)} %convert_element_type.32, f32[2,384]{1,0:T(2,128)S(1)} %convert_add_fusion, f32[1,64,256,16]{2,3,1,0:T(8,128)} %get-tuple-element.10, f32[64,256,16]{1,2,0:T(8,128)} %add_subtract_fusion.1, f32[64,256,16]{1,2,0:T(8,128)S(1)} %copy-done.1, ...), kind=kOutput, calls=%fused_computation.37 | convolution fusion | flops 945291264 | bytes 5273600 | tf_op jit(solution)/shard_map/kbnd,dc->kbnc/dot_general | solution.py:11
  518.4 12.0 %collective-permute-done.18 = f32[64,256,16]{1,2,0:T(8,128)S(1)} collective-permute-done((f32[64,256,16]{1,2,0:T(8,128)S(1)}, f32[64,256,16]{1,2,0:T(8,128)S(1)}, u32[]{:S(2)}, u32[]{:S(2)}) %collective-permute-start.18) | collective-permute-done | bytes 1048608 | tf_op jit(solution)/shard_map/ppermute | solution.py:28
  531.2 6.9 %collective-permute-start.19 = (f32[64,256,16]{1,2,0:T(8,128)S(1)}, f32[64,256,16]{1,2,0:T(8,128)S(1)}, u32[]{:S(2)}, u32[]{:S(2)}) collective-permute-start(f32[64,256,16]{1,2,0:T(8,128)S(1)} %get-tuple-element.5), channel_id=1, source_target_pairs={{0,1},{1,2},{2,3},{3,4},{4,5},{5,6},{6,7},{7,8},{8,9},{9,10},{10,1... | collective-permute-start | bytes 3145736 | tf_op jit(solution)/shard_map/ppermute | solution.py:36
  538.1 9.4 %collective-permute-done.19 = f32[64,256,16]{1,2,0:T(8,128)S(1)} collective-permute-done((f32[64,256,16]{1,2,0:T(8,128)S(1)}, f32[64,256,16]{1,2,0:T(8,128)S(1)}, u32[]{:S(2)}, u32[]{:S(2)}) %collective-permute-start.19) | collective-permute-done | bytes 1048608 | tf_op jit(solution)/shard_map/ppermute | solution.py:36
  547.8 8.7 %collective-permute-start.20 = (f32[64,256,16]{1,2,0:T(8,128)S(1)}, f32[64,256,16]{1,2,0:T(8,128)S(1)}, u32[]{:S(2)}, u32[]{:S(2)}) collective-permute-start(f32[64,256,16]{1,2,0:T(8,128)S(1)} %fusion.124), channel_id=1, source_target_pairs={{0,2},{1,3},{2,4},{3,5},{4,6},{5,7},{6,8},{7,9},{8,10},{9,11},{10,... | collective-permute-start | bytes 3145736 | tf_op jit(solution)/shard_map/ppermute | solution.py:36
  556.5 18.6 %collective-permute-done.20 = f32[64,256,16]{1,2,0:T(8,128)S(1)} collective-permute-done((f32[64,256,16]{1,2,0:T(8,128)S(1)}, f32[64,256,16]{1,2,0:T(8,128)S(1)}, u32[]{:S(2)}, u32[]{:S(2)}) %collective-permute-start.20) | collective-permute-done | bytes 1048608 | tf_op jit(solution)/shard_map/ppermute | solution.py:36
  575.4 3.4 collective-permute-start.21
  578.8 25.7 %collective-permute-done.21 = f32[64,256,16]{1,2,0:T(8,128)S(1)} collective-permute-done((f32[64,256,16]{1,2,0:T(8,128)S(1)}, f32[64,256,16]{1,2,0:T(8,128)S(1)}, u32[]{:S(2)}, u32[]{:S(2)}) %collective-permute-start.21) | collective-permute-done | bytes 1048608 | tf_op jit(solution)/shard_map/ppermute | solution.py:36
  604.7 2.7 collective-permute-start.22
  607.4 20.7 %collective-permute-done.22 = f32[64,256,16]{1,2,0:T(8,128)S(1)} collective-permute-done((f32[64,256,16]{1,2,0:T(8,128)S(1)}, f32[64,256,16]{1,2,0:T(8,128)S(1)}, u32[]{:S(2)}, u32[]{:S(2)}) %collective-permute-start.22) | collective-permute-done | bytes 1048608 | tf_op jit(solution)/shard_map/ppermute | solution.py:36
  628.4 8.3 %collective-permute-start.23 = (f32[64,256,16]{1,2,0:T(8,128)S(1)}, f32[64,256,16]{1,2,0:T(8,128)S(1)}, u32[]{:S(2)}, u32[]{:S(2)}) collective-permute-start(f32[64,256,16]{1,2,0:T(8,128)S(1)} %add.241), channel_id=1, source_target_pairs={{0,16},{1,17},{2,18},{3,19},{4,20},{5,21},{6,22},{7,23},{8,24},{9,... | collective-permute-start | bytes 3145736 | tf_op jit(solution)/shard_map/ppermute | solution.py:36
  636.6 20.6 %collective-permute-done.23 = f32[64,256,16]{1,2,0:T(8,128)S(1)} collective-permute-done((f32[64,256,16]{1,2,0:T(8,128)S(1)}, f32[64,256,16]{1,2,0:T(8,128)S(1)}, u32[]{:S(2)}, u32[]{:S(2)}) %collective-permute-start.23) | collective-permute-done | bytes 1048608 | tf_op jit(solution)/shard_map/ppermute | solution.py:36
  (49 shorter events, 29.2 us)
Async XLA Ops:
  0.0 1.4 copy-start
  1.4 4.7 copy-start.2
  25.3 2.3 copy-start.3
  25.5 14.4 %collective-permute-start = (f32[64,256,16]{1,2,0:T(8,128)S(1)}, f32[64,256,16]{1,2,0:T(8,128)S(1)}, u32[]{:S(2)}, u32[]{:S(2)}) collective-permute-start(f32[64,256,16]{1,2,0:T(8,128)S(1)} %get-tuple-element.20), channel_id=1, source_target_pairs={{1,0},{2,1},{3,2},{4,3},{5,4},{6,5},{7,6},{8,7},{9,8},{10,9},{11,1... | collective-permute-start | bytes 3145736 | tf_op jit(solution)/shard_map/ppermute | solution.py:28
  41.7 16.3 %collective-permute-start.1 = (f32[64,256,16]{1,2,0:T(8,128)S(1)}, f32[64,256,16]{1,2,0:T(8,128)S(1)}, u32[]{:S(2)}, u32[]{:S(2)}) collective-permute-start(f32[64,256,16]{1,2,0:T(8,128)S(1)} %get-tuple-element.17), channel_id=1, source_target_pairs={{0,1},{1,2},{2,3},{3,4},{4,5},{5,6},{6,7},{7,8},{8,9},{9,10},{10,1... | collective-permute-start | bytes 3145736 | tf_op jit(solution)/shard_map/ppermute | solution.py:36
  58.2 27.9 %collective-permute-start.2 = (f32[64,256,16]{1,2,0:T(8,128)S(1)}, f32[64,256,16]{1,2,0:T(8,128)S(1)}, u32[]{:S(2)}, u32[]{:S(2)}) collective-permute-start(f32[64,256,16]{1,2,0:T(8,128)S(1)} %fusion.121), channel_id=1, source_target_pairs={{0,2},{1,3},{2,4},{3,5},{4,6},{5,7},{6,8},{7,9},{8,10},{9,11},{10,... | collective-permute-start | bytes 3145736 | tf_op jit(solution)/shard_map/ppermute | solution.py:36
  86.3 28.8 %collective-permute-start.3 = (f32[64,256,16]{1,2,0:T(8,128)S(1)}, f32[64,256,16]{1,2,0:T(8,128)S(1)}, u32[]{:S(2)}, u32[]{:S(2)}) collective-permute-start(f32[64,256,16]{1,2,0:T(8,128)S(1)} %add.203), channel_id=1, source_target_pairs={{0,4},{1,5},{2,6},{3,7},{4,8},{5,9},{6,10},{7,11},{8,12},{9,13},{1... | collective-permute-start | bytes 3145736 | tf_op jit(solution)/shard_map/ppermute | solution.py:36
  115.3 25.6 %collective-permute-start.4 = (f32[64,256,16]{1,2,0:T(8,128)S(1)}, f32[64,256,16]{1,2,0:T(8,128)S(1)}, u32[]{:S(2)}, u32[]{:S(2)}) collective-permute-start(f32[64,256,16]{1,2,0:T(8,128)S(1)} %add.204), channel_id=1, source_target_pairs={{0,8},{1,9},{2,10},{3,11},{4,12},{5,13},{6,14},{7,15},{8,16},{9,17... | collective-permute-start | bytes 3145736 | tf_op jit(solution)/shard_map/ppermute | solution.py:36
  141.2 29.1 %copy-start.1 = (f32[64,256,16]{1,2,0:T(8,128)S(1)}, f32[64,256,16]{1,2,0:T(8,128)}, u32[]{:S(2)}) copy-start(f32[64,256,16]{1,2,0:T(8,128)} %param.6) | copy-start | bytes 3145732
  141.2 27.7 %collective-permute-start.5 = (f32[64,256,16]{1,2,0:T(8,128)S(1)}, f32[64,256,16]{1,2,0:T(8,128)S(1)}, u32[]{:S(2)}, u32[]{:S(2)}) collective-permute-start(f32[64,256,16]{1,2,0:T(8,128)S(1)} %add.205), channel_id=1, source_target_pairs={{0,16},{1,17},{2,18},{3,19},{4,20},{5,21},{6,22},{7,23},{8,24},{9,... | collective-permute-start | bytes 3145736 | tf_op jit(solution)/shard_map/ppermute | solution.py:36
  192.5 14.2 %collective-permute-start.6 = (f32[64,256,16]{1,2,0:T(8,128)S(1)}, f32[64,256,16]{1,2,0:T(8,128)S(1)}, u32[]{:S(2)}, u32[]{:S(2)}) collective-permute-start(f32[64,256,16]{1,2,0:T(8,128)S(1)} %get-tuple-element.16), channel_id=1, source_target_pairs={{1,0},{2,1},{3,2},{4,3},{5,4},{6,5},{7,6},{8,7},{9,8},{10,9},{11,1... | collective-permute-start | bytes 3145736 | tf_op jit(solution)/shard_map/ppermute | solution.py:28
  208.5 16.3 %collective-permute-start.7 = (f32[64,256,16]{1,2,0:T(8,128)S(1)}, f32[64,256,16]{1,2,0:T(8,128)S(1)}, u32[]{:S(2)}, u32[]{:S(2)}) collective-permute-start(f32[64,256,16]{1,2,0:T(8,128)S(1)} %get-tuple-element.13), channel_id=1, source_target_pairs={{0,1},{1,2},{2,3},{3,4},{4,5},{5,6},{6,7},{7,8},{8,9},{9,10},{10,1... | collective-permute-start | bytes 3145736 | tf_op jit(solution)/shard_map/ppermute | solution.py:36
  225.1 25.4 %collective-permute-start.8 = (f32[64,256,16]{1,2,0:T(8,128)S(1)}, f32[64,256,16]{1,2,0:T(8,128)S(1)}, u32[]{:S(2)}, u32[]{:S(2)}) collective-permute-start(f32[64,256,16]{1,2,0:T(8,128)S(1)} %fusion.122), channel_id=1, source_target_pairs={{0,2},{1,3},{2,4},{3,5},{4,6},{5,7},{6,8},{7,9},{8,10},{9,11},{10,... | collective-permute-start | bytes 3145736 | tf_op jit(solution)/shard_map/ppermute | solution.py:36
  250.7 26.3 %collective-permute-start.9 = (f32[64,256,16]{1,2,0:T(8,128)S(1)}, f32[64,256,16]{1,2,0:T(8,128)S(1)}, u32[]{:S(2)}, u32[]{:S(2)}) collective-permute-start(f32[64,256,16]{1,2,0:T(8,128)S(1)} %add.215), channel_id=1, source_target_pairs={{0,4},{1,5},{2,6},{3,7},{4,8},{5,9},{6,10},{7,11},{8,12},{9,13},{1... | collective-permute-start | bytes 3145736 | tf_op jit(solution)/shard_map/ppermute | solution.py:36
  277.2 24.6 %collective-permute-start.10 = (f32[64,256,16]{1,2,0:T(8,128)S(1)}, f32[64,256,16]{1,2,0:T(8,128)S(1)}, u32[]{:S(2)}, u32[]{:S(2)}) collective-permute-start(f32[64,256,16]{1,2,0:T(8,128)S(1)} %add.216), channel_id=1, source_target_pairs={{0,8},{1,9},{2,10},{3,11},{4,12},{5,13},{6,14},{7,15},{8,16},{9,17... | collective-permute-start | bytes 3145736 | tf_op jit(solution)/shard_map/ppermute | solution.py:36
  302.0 23.3 %collective-permute-start.11 = (f32[64,256,16]{1,2,0:T(8,128)S(1)}, f32[64,256,16]{1,2,0:T(8,128)S(1)}, u32[]{:S(2)}, u32[]{:S(2)}) collective-permute-start(f32[64,256,16]{1,2,0:T(8,128)S(1)} %add.217), channel_id=1, source_target_pairs={{0,16},{1,17},{2,18},{3,19},{4,20},{5,21},{6,22},{7,23},{8,24},{9,... | collective-permute-start | bytes 3145736 | tf_op jit(solution)/shard_map/ppermute | solution.py:36
  348.9 14.2 %collective-permute-start.12 = (f32[64,256,16]{1,2,0:T(8,128)S(1)}, f32[64,256,16]{1,2,0:T(8,128)S(1)}, u32[]{:S(2)}, u32[]{:S(2)}) collective-permute-start(f32[64,256,16]{1,2,0:T(8,128)S(1)} %get-tuple-element.12), channel_id=1, source_target_pairs={{1,0},{2,1},{3,2},{4,3},{5,4},{6,5},{7,6},{8,7},{9,8},{10,9},{11,1... | collective-permute-start | bytes 3145736 | tf_op jit(solution)/shard_map/ppermute | solution.py:28
  364.9 16.3 %collective-permute-start.13 = (f32[64,256,16]{1,2,0:T(8,128)S(1)}, f32[64,256,16]{1,2,0:T(8,128)S(1)}, u32[]{:S(2)}, u32[]{:S(2)}) collective-permute-start(f32[64,256,16]{1,2,0:T(8,128)S(1)} %get-tuple-element.9), channel_id=1, source_target_pairs={{0,1},{1,2},{2,3},{3,4},{4,5},{5,6},{6,7},{7,8},{8,9},{9,10},{10,1... | collective-permute-start | bytes 3145736 | tf_op jit(solution)/shard_map/ppermute | solution.py:36
  381.5 28.5 %collective-permute-start.14 = (f32[64,256,16]{1,2,0:T(8,128)S(1)}, f32[64,256,16]{1,2,0:T(8,128)S(1)}, u32[]{:S(2)}, u32[]{:S(2)}) collective-permute-start(f32[64,256,16]{1,2,0:T(8,128)S(1)} %fusion.123), channel_id=1, source_target_pairs={{0,2},{1,3},{2,4},{3,5},{4,6},{5,7},{6,8},{7,9},{8,10},{9,11},{10,... | collective-permute-start | bytes 3145736 | tf_op jit(solution)/shard_map/ppermute | solution.py:36
  410.2 28.7 %collective-permute-start.15 = (f32[64,256,16]{1,2,0:T(8,128)S(1)}, f32[64,256,16]{1,2,0:T(8,128)S(1)}, u32[]{:S(2)}, u32[]{:S(2)}) collective-permute-start(f32[64,256,16]{1,2,0:T(8,128)S(1)} %add.227), channel_id=1, source_target_pairs={{0,4},{1,5},{2,6},{3,7},{4,8},{5,9},{6,10},{7,11},{8,12},{9,13},{1... | collective-permute-start | bytes 3145736 | tf_op jit(solution)/shard_map/ppermute | solution.py:36
  439.1 25.5 %collective-permute-start.16 = (f32[64,256,16]{1,2,0:T(8,128)S(1)}, f32[64,256,16]{1,2,0:T(8,128)S(1)}, u32[]{:S(2)}, u32[]{:S(2)}) collective-permute-start(f32[64,256,16]{1,2,0:T(8,128)S(1)} %add.228), channel_id=1, source_target_pairs={{0,8},{1,9},{2,10},{3,11},{4,12},{5,13},{6,14},{7,15},{8,16},{9,17... | collective-permute-start | bytes 3145736 | tf_op jit(solution)/shard_map/ppermute | solution.py:36
  464.8 27.8 %collective-permute-start.17 = (f32[64,256,16]{1,2,0:T(8,128)S(1)}, f32[64,256,16]{1,2,0:T(8,128)S(1)}, u32[]{:S(2)}, u32[]{:S(2)}) collective-permute-start(f32[64,256,16]{1,2,0:T(8,128)S(1)} %add.229), channel_id=1, source_target_pairs={{0,16},{1,17},{2,18},{3,19},{4,20},{5,21},{6,22},{7,23},{8,24},{9,... | collective-permute-start | bytes 3145736 | tf_op jit(solution)/shard_map/ppermute | solution.py:36
  516.2 14.2 %collective-permute-start.18 = (f32[64,256,16]{1,2,0:T(8,128)S(1)}, f32[64,256,16]{1,2,0:T(8,128)S(1)}, u32[]{:S(2)}, u32[]{:S(2)}) collective-permute-start(f32[64,256,16]{1,2,0:T(8,128)S(1)} %get-tuple-element.8), channel_id=1, source_target_pairs={{1,0},{2,1},{3,2},{4,3},{5,4},{6,5},{7,6},{8,7},{9,8},{10,9},{11,1... | collective-permute-start | bytes 3145736 | tf_op jit(solution)/shard_map/ppermute | solution.py:28
  531.2 16.3 %collective-permute-start.19 = (f32[64,256,16]{1,2,0:T(8,128)S(1)}, f32[64,256,16]{1,2,0:T(8,128)S(1)}, u32[]{:S(2)}, u32[]{:S(2)}) collective-permute-start(f32[64,256,16]{1,2,0:T(8,128)S(1)} %get-tuple-element.5), channel_id=1, source_target_pairs={{0,1},{1,2},{2,3},{3,4},{4,5},{5,6},{6,7},{7,8},{8,9},{9,10},{10,1... | collective-permute-start | bytes 3145736 | tf_op jit(solution)/shard_map/ppermute | solution.py:36
  547.8 27.4 %collective-permute-start.20 = (f32[64,256,16]{1,2,0:T(8,128)S(1)}, f32[64,256,16]{1,2,0:T(8,128)S(1)}, u32[]{:S(2)}, u32[]{:S(2)}) collective-permute-start(f32[64,256,16]{1,2,0:T(8,128)S(1)} %fusion.124), channel_id=1, source_target_pairs={{0,2},{1,3},{2,4},{3,5},{4,6},{5,7},{6,8},{7,9},{8,10},{9,11},{10,... | collective-permute-start | bytes 3145736 | tf_op jit(solution)/shard_map/ppermute | solution.py:36
  575.4 29.1 %collective-permute-start.21 = (f32[64,256,16]{1,2,0:T(8,128)S(1)}, f32[64,256,16]{1,2,0:T(8,128)S(1)}, u32[]{:S(2)}, u32[]{:S(2)}) collective-permute-start(f32[64,256,16]{1,2,0:T(8,128)S(1)} %add.239), channel_id=1, source_target_pairs={{0,4},{1,5},{2,6},{3,7},{4,8},{5,9},{6,10},{7,11},{8,12},{9,13},{1... | collective-permute-start | bytes 3145736 | tf_op jit(solution)/shard_map/ppermute | solution.py:36
  604.7 23.5 %collective-permute-start.22 = (f32[64,256,16]{1,2,0:T(8,128)S(1)}, f32[64,256,16]{1,2,0:T(8,128)S(1)}, u32[]{:S(2)}, u32[]{:S(2)}) collective-permute-start(f32[64,256,16]{1,2,0:T(8,128)S(1)} %add.240), channel_id=1, source_target_pairs={{0,8},{1,9},{2,10},{3,11},{4,12},{5,13},{6,14},{7,15},{8,16},{9,17... | collective-permute-start | bytes 3145736 | tf_op jit(solution)/shard_map/ppermute | solution.py:36
  628.4 28.9 %collective-permute-start.23 = (f32[64,256,16]{1,2,0:T(8,128)S(1)}, f32[64,256,16]{1,2,0:T(8,128)S(1)}, u32[]{:S(2)}, u32[]{:S(2)}) collective-permute-start(f32[64,256,16]{1,2,0:T(8,128)S(1)} %add.241), channel_id=1, source_target_pairs={{0,16},{1,17},{2,18},{3,19},{4,20},{5,21},{6,22},{7,23},{8,24},{9,... | collective-permute-start | bytes 3145736 | tf_op jit(solution)/shard_map/ppermute | solution.py:36
where the time goes:
time: 669 us; the launch traced here: 660 us
  waiting for transfers between devices  431 us (64%)
  starting transfers between devices  120 us (18%)
  matrix products  89.9 us (13%)
  other arithmetic  13.4 us (2%)
    ppermute x20, waiting for transfers between devices, local(): lax.ppermute(inclusive, 'time', [(source, source + distance) for source i...  393 us
    ppermute x20, starting transfers between devices, local(): lax.ppermute(inclusive, 'time', [(source, source + distance) for source i...  102 us
    dot_general x4, matrix products, drift_block(): jnp.einsum('kbnd,dc->kbnc', hidden_act.astype(jnp.bfloat16), w_out, prefe...  85.2 us
    ppermute x4, waiting for transfers between devices, local(): next_first = lax.ppermute(drifts[0], 'time', from_next)  38.6 us
    ppermute x4, starting transfers between devices, local(): next_first = lax.ppermute(drifts[0], 'time', from_next)  18.5 us
  transfers between devices with their start and end apart: 24, of which 24 were waited for; matrix products, arithmetic and copies ran while one was open for 0% of the time, Pallas kernels for 0%

commit v1 on v0

v1 whole, which is shorter than its diff:
```python
import functools
import math

import jax
import jax.numpy as jnp
from jax import lax
from jax.experimental import pallas as pl
from jax.experimental.pallas import tpu as pltpu
from jax.sharding import PartitionSpec as P

SWEEPS = 4
UNROLL = 8
LANES = 128
C1 = 2.0 * math.sqrt(2.0 / math.pi)
C3 = 8.0 * math.sqrt(2.0 / math.pi) * 0.044715


def compute_kernel(x_ref, scale_ref, shift_ref, w_in_ref, w_out_ref, step_ref, out_ref, w_scr, xs_scr):
    steps = scale_ref.shape[0]
    hidden = scale_ref.shape[1]
    batch, chans, tokens = x_ref.shape
    f32, bf16 = jnp.float32, jnp.bfloat16

    row = lax.broadcasted_iota(jnp.int32, (LANES, LANES), 0)
    lane = lax.broadcasted_iota(jnp.int32, (LANES, LANES), 1)
    eye = (row == lane).astype(f32).astype(bf16)
    mods = jnp.concatenate([scale_ref[...], shift_ref[...]], axis=0)
    tdims = (((0,), (0,)), ((), ()))
    mods_t = lax.dot_general(mods, eye, tdims, preferred_element_type=f32).astype(bf16)
    spread = ((lane % chans == row) & (lane < 3 * chans) & (row < chans)).astype(f32).astype(bf16)
    w3 = 0.5 * lax.dot_general(w_in_ref[...], spread[:chans], tdims, preferred_element_type=f32)
    lane_row = lax.broadcasted_iota(jnp.int32, (1, LANES), 1)
    w3 = w3 + jnp.where(lane_row == 3 * chans, 0.5, 0.0)
    ones = jnp.where(lane_row < 3 * chans, 1.0, 0.0)
    use_hi = (lane_row < chans) | (lane_row >= 3 * chans)
    use_mid = lane_row < 2 * chans

    @pl.loop(0, steps)
    def _(j):
        pick = ((row == j) & (lane < 3 * chans)) | ((row == steps + j) & (lane == 3 * chans))
        picked = jnp.dot(mods_t, pick.astype(f32).astype(bf16), preferred_element_type=f32)
        prod = w3 * (picked + ones)
        hi = prod.astype(bf16).astype(f32)
        rest = prod - hi
        mid = rest.astype(bf16).astype(f32)
        piece = jnp.where(use_hi, hi, jnp.where(use_mid, mid, rest - mid))
        w_scr[j] = piece.astype(bf16)

    w_out_t = w_out_ref[...]
    pad_rows = LANES - 4 * chans
    ones_rows = jnp.ones((chans, tokens), bf16)
    zero_rows = jnp.zeros((pad_rows, tokens), bf16)
    groups = steps // UNROLL

    for b in range(batch):
        x0 = x_ref[b]
        x0_bf = x0.astype(bf16)

        @pl.loop(0, steps)
        def _(j):
            xs_scr[j] = x0_bf

        def body(g, carry):
            d_prev, total = carry
            j0 = lax.rem(g, groups) * UNROLL
            for u in range(UNROLL):
                j = j0 + u
                x = xs_scr[j]
                rhs = jnp.concatenate([x, x, x, ones_rows, zero_rows], axis=0)
                half = jnp.dot(w_scr[j], rhs, preferred_element_type=f32)
                arg = half * (half * half * C3 + C1)
                hid = (half * (1.0 + jnp.tanh(arg))).astype(bf16)
                d = jnp.dot(w_out_t, hid, preferred_element_type=f32)
                if u == 0:
                    inc = step_ref[jnp.maximum(j - 1, 0)] * (0.5 * (d_prev + d))
                    total = jnp.where(j0 == 0, 0.0, total + inc)
                else:
                    total = total + step_ref[j - 1] * (0.5 * (d_prev + d))
                new = x0 + total
                xs_scr[j] = new.astype(bf16)
                out_ref[j, b] = new
                d_prev = d
            return d_prev, total

        zero = jnp.zeros((chans, tokens), f32)
        lax.fori_loop(0, SWEEPS * groups, body, (zero, zero))


def solution(mesh):
    n_time = mesh.shape["time"]

    def local(x_init, w_in, w_out, mod_scale, mod_shift, step_size):
        batch, tokens, chans = x_init.shape
        hidden = w_in.shape[1]
        share = batch // n_time
        me = lax.axis_index("time")
        scale = lax.all_gather(mod_scale, "time", tiled=True)
        shift = lax.all_gather(mod_shift, "time", tiled=True)
        step = lax.all_gather(step_size, "time", tiled=True)
        steps = scale.shape[0]
        x_t = jnp.swapaxes(x_init, 1, 2)
        x_mine = lax.dynamic_slice_in_dim(x_t, me * share, share, 0)
        vmem = pl.BlockSpec(memory_space=pltpu.VMEM)
        out = pl.pallas_call(
            compute_kernel,
            out_shape=jax.ShapeDtypeStruct((steps, share, chans, tokens), jnp.float32),
            in_specs=[vmem] * 5 + [pl.BlockSpec(memory_space=pltpu.SMEM)],
            out_specs=vmem,
            scratch_shapes=[
                pltpu.VMEM((steps, hidden, LANES), jnp.bfloat16),
                pltpu.VMEM((steps, chans, tokens), jnp.bfloat16),
            ],
            compiler_params=pltpu.CompilerParams(vmem_limit_bytes=48 * 1024 * 1024),
            name="sweeps",
        )(x_mine, scale, shift, w_in, w_out.T, step)
        out = lax.all_to_all(out, "time", split_axis=0, concat_axis=1, tiled=True)
        return jnp.swapaxes(out, 2, 3)

    return jax.shard_map(local, mesh=mesh, in_specs=(P("data"), P(), P(), P("time"), P("time"), P("time")), out_specs=P("time", "data"), check_vma=False)
```

time: 669 us -> 296 us (0.44)
  the two profiles are of different devices: /device:TPU:102 before, /device:TPU:97 now
where the time goes in v1:
time: 296 us
  blocking collectives  148 us (50%)
  Pallas kernels  144 us (49%)
  local copies, waits for them, and re-layouts  3.9 us (1%)
    pallas_call x1, Pallas kernels, local(): pl.pallas_call(compute_kernel, out_shape=jax.ShapeDtypeStruct((steps, sha...  144 us
    unnamed x1, blocking collectives  49.8 us
    all_to_all x1, blocking collectives, local(): out = lax.all_to_all(out, 'time', split_axis=0, concat_axis=1, tiled=True)  39 us
    all_gather x1, blocking collectives, local(): shift = lax.all_gather(mod_shift, 'time', tiled=True)  32.3 us
    all_gather x1, blocking collectives, local(): scale = lax.all_gather(mod_scale, 'time', tiled=True)  26.8 us

profile of v1, /device:TPU:97, one launch (start us, length us, event | category | flops | bytes accessed | tf_op | source)
XLA Modules:
  0.0 295.8 jit_solution(9014963851389041430)
XLA Ops:
  0.0 0.0 copy-start
  0.0 0.9 dynamic-update-slice
  0.9 49.8 %all-reduce.step_ref = f32[64]{0:T(128)S(1)} all-reduce(f32[64]{0:T(128)S(1)} %dynamic-update-slice), channel_id=1, replica_groups=mesh['data'=1,'time'=32] {'time'}, use_global_device_ids=true, to_apply=%add | all-reduce | flops 64 | bytes 512
  50.7 26.8 %all-gather = bf16[32,2,384]{2,1,0:T(2,128)(2,1)S(1)} all-gather(bf16[1,2,384]{2,1,0:T(2,128)(2,1)} %bitcast.13), channel_id=1, replica_groups=mesh['data'=1,'time'=32] {'time'}, dimensions={0}, use_global_device_ids=true | all-gather | bytes 50688 | tf_op jit(solution)/shard_map/all_gather | solution.py:97
  77.5 32.3 %all-gather.1 = bf16[32,2,384]{2,1,0:T(2,128)(2,1)S(1)} all-gather(bf16[1,2,384]{2,1,0:T(2,128)(2,1)} %bitcast.14), channel_id=1, replica_groups=mesh['data'=1,'time'=32] {'time'}, dimensions={0}, use_global_device_ids=true | all-gather | bytes 50688 | tf_op jit(solution)/shard_map/all_gather | solution.py:98
  109.9 0.0 copy-done
  109.9 0.0 copy-start.1
  109.9 0.7 copy-done.1
  110.6 0.0 copy-start.2
  110.6 0.7 copy-done.2
  111.3 144.0 %sweeps.1 = f32[64,2,16,256]{3,2,1,0:T(8,128)S(1)} custom-call(f32[2,16,256]{2,1,0:T(8,128)S(1)} %dynamic-slice_bitcast_fusion.x_ref, bf16[64,384]{1,0:T(8,128)(2,1)S(1)} %reshape.3.scale_ref, bf16[64,384]{1,0:T(8,128)(2,1)S(1)} %reshape.5.shift_ref, bf16[16,384]{1,0:T(8,128)(2,1)S(1)} %copy-done.1, bf16[16,384]{1,0:T(8,128)(2,1)S(1)} %bitcast.11, ...), custom_call_target="tpu_custom_call" | custom-call | tf_op jit(solution)/shard_map/sweeps/pallas_call | solution.py:104
  255.3 39.0 %all_to_all.18 = f32[64,2,16,256]{3,2,1,0:T(8,128)S(1)} all-to-all(f32[64,2,16,256]{3,2,1,0:T(8,128)S(1)} %sweeps.1), channel_id=1, replica_groups=mesh['data'=1,'time'=32] {'time'}, dimensions={0} | all-to-all | bytes 4194304 | tf_op jit(solution)/shard_map/all_to_all | solution.py:116
  294.3 1.5 copy.8
  (4 shorter events, 0.1 us)
Async XLA Ops:
  0.0 109.9 %copy-start = (f32[64,256,16]{1,2,0:T(8,128)S(1)}, f32[64,256,16]{1,2,0:T(8,128)}, u32[]{:S(2)}) copy-start(f32[64,256,16]{1,2,0:T(8,128)} %param.6) | copy-start | bytes 3145732
  109.9 0.7 copy-start.1
  110.6 0.7 copy-start.2

commit v2 on v0

v2 whole, which is shorter than its diff:
```python
import functools
import math

import jax
import jax.numpy as jnp
from jax import lax
from jax.experimental import pallas as pl
from jax.experimental.pallas import tpu as pltpu
from jax.sharding import PartitionSpec as P

SWEEPS = 4
UNROLL = 16
AHEAD = 2
LANES = 128
FOLD_LIMIT = 2.0 ** 60
C1 = 2.0 * math.sqrt(2.0 / math.pi)
C3 = 8.0 * math.sqrt(2.0 / math.pi) * 0.044715
F32, BF16 = jnp.float32, jnp.bfloat16
MESH = pl.DeviceIdType.MESH
CONTRACT0 = (((0,), (0,)), ((), ()))


def signal_all(n, me):
    barrier = pltpu.get_barrier_semaphore()

    @pl.loop(1, n)
    def _(i):
        pl.semaphore_signal(barrier, inc=1, device_id={"time": lax.rem(me + i, n)}, device_id_type=MESH)


def one_hot(cond):
    return jnp.where(cond, 1.0, 0.0).astype(BF16)


def gather_kernel(n, scale_ref, shift_ref, step_ref, w_in_ref, mods_t_ref, steps_ref, flag_ref, mine, mine_step, mods, send_sem, recv_sem):
    me = lax.axis_index("time")
    signal_all(n, me)
    per = scale_ref.shape[0]
    mine[0:per] = scale_ref[...]
    mine[per:2 * per] = shift_ref[...]
    lane = lax.broadcasted_iota(jnp.int32, (1, LANES), 1)
    row = jnp.zeros((1, LANES), F32)
    for i in range(per):
        row = jnp.where(lane == i, step_ref[i], row)
    mine_step[...] = row
    pl.semaphore_wait(pltpu.get_barrier_semaphore(), n - 1)

    def copies(i):
        to = {"time": lax.rem(me + i, n)}
        return (
            pltpu.make_async_remote_copy(mine, mods.at[me], send_sem.at[0, i], recv_sem.at[0, i], device_id=to, device_id_type=MESH),
            pltpu.make_async_remote_copy(mine_step, steps_ref.at[me], send_sem.at[1, i], recv_sem.at[1, i], device_id=to, device_id_type=MESH),
        )

    @pl.loop(1, n)
    def _(i):
        for c in copies(i):
            c.start()

    mods[me] = mine[...]
    steps_ref[me] = mine_step[...]

    @pl.loop(1, n)
    def _(i):
        for c in copies(i):
            c.wait()

    parts = [mods[q].astype(F32) for q in range(n)]
    flat = jnp.concatenate(parts, axis=0).astype(BF16)
    r = lax.broadcasted_iota(jnp.int32, (LANES, LANES), 0)
    c = lax.broadcasted_iota(jnp.int32, (LANES, LANES), 1)
    mods_t_ref[...] = lax.dot_general(flat, one_hot(r == c), CONTRACT0, preferred_element_type=F32).astype(BF16)
    top = 0.0
    for q in range(n):
        top = jnp.maximum(top, jnp.abs(1.0 + parts[q][:per]))
    bound = jnp.max(top) * jnp.max(jnp.abs(w_in_ref[...].astype(F32)))
    flag_ref[0] = (bound <= FOLD_LIMIT).astype(jnp.int32)


def scale_row(j, per):
    return j // per * (2 * per) + lax.rem(j, per)


def sweeps_kernel(n, per, fold, x_ref, mods_t_ref, w_in_ref, w_out_ref, step_ref, out_ref, w_scr, xs_scr, res_scr, send_sem, recv_sem):
    me = lax.axis_index("time")
    signal_all(n, me)
    share, chans, tokens = x_ref.shape
    steps = n * per
    mods_t = mods_t_ref[...]

    row = lax.broadcasted_iota(jnp.int32, (LANES, LANES), 0)
    lane = lax.broadcasted_iota(jnp.int32, (LANES, LANES), 1)
    lane_row = lax.broadcasted_iota(jnp.int32, (1, LANES), 1)
    spread = one_hot((lane % chans == row) & (lane < 3 * chans))
    w3 = 0.5 * lax.dot_general(w_in_ref[...], spread[:chans], CONTRACT0, preferred_element_type=F32)

    if fold:
        w3 = w3 + jnp.where(lane_row == 3 * chans, 0.5, 0.0)
        ones = jnp.where(lane_row < 3 * chans, 1.0, 0.0)
        use_hi = (lane_row < chans) | (lane_row >= 3 * chans)
        use_mid = lane_row < 2 * chans

        @pl.loop(0, steps)
        def _(j):
            src = scale_row(j, per)
            pick = ((row == src) & (lane < 3 * chans)) | ((row == src + per) & (lane == 3 * chans))
            picked = jnp.dot(mods_t, one_hot(pick), preferred_element_type=F32)
            prod = w3 * (picked + ones)
            hi = prod.astype(BF16).astype(F32)
            rest = prod - hi
            mid = rest.astype(BF16).astype(F32)
            w_scr[j] = jnp.where(use_hi, hi, jnp.where(use_mid, mid, rest - mid)).astype(BF16)
    else:
        w_scr[0] = (w3 * jnp.where(lane_row < chans, 2.0, 0.0)).astype(BF16)

    w_out_t = w_out_ref[...]
    ones_rows = jnp.ones((chans, tokens), BF16)
    zero_rows = jnp.zeros((LANES - 4 * chans, tokens), BF16)
    row_tok = lax.broadcasted_iota(jnp.int32, (LANES, tokens), 0)
    unroll = UNROLL if fold else per
    groups = steps // unroll

    def half_pre(j, x):
        rhs = jnp.concatenate([x, x, x, ones_rows, zero_rows], axis=0)
        if fold:
            return jnp.dot(w_scr[j], rhs, preferred_element_type=F32)
        u = jnp.dot(w_scr[0], rhs, preferred_element_type=F32)
        src = scale_row(j, per)
        scale = jnp.dot(mods_t, one_hot(row_tok == src), preferred_element_type=F32)
        shift = jnp.dot(mods_t, one_hot(row_tok == src + per), preferred_element_type=F32)
        return 0.5 * (u * (1.0 + scale) + shift)

    def copy(b, i):
        q = lax.rem(me + i, n)
        return pltpu.make_async_remote_copy(
            res_scr.at[pl.ds(q * per, per), b], out_ref.at[:, me * share + b], send_sem.at[b, i], recv_sem.at[b, i],
            device_id={"time": q}, device_id_type=MESH)

    for b in range(share):
        x0 = x_ref[b]
        x0_bf = x0.astype(BF16)

        @pl.loop(0, steps)
        def _(j):
            xs_scr[j] = x0_bf

        def body(g, carry):
            d_prev, total = carry
            j0 = lax.rem(g, groups) * unroll
            xs = [xs_scr[j0 + u] for u in range(unroll)]
            halves, ds = {}, []
            for u in range(unroll + AHEAD):
                if u < unroll:
                    halves[u] = half_pre(j0 + u, xs[u])
                if u >= AHEAD:
                    half = halves.pop(u - AHEAD)
                    arg = half * (half * half * C3 + C1)
                    hidden = (half * (1.0 + jnp.tanh(arg))).astype(BF16)
                    ds.append(jnp.dot(w_out_t, hidden, preferred_element_type=F32))
            for u in range(unroll):
                j = j0 + u
                d = ds[u]
                i = jnp.maximum(j - 1, 0)
                inc = step_ref[i // per, 0, lax.rem(i, per)] * (0.5 * (d_prev + d))
                total = total + inc
                if u == 0:
                    total = jnp.where(j0 == 0, 0.0, total)
                new = x0 + total
                xs_scr[j] = new.astype(BF16)
                res_scr[j, b] = new
                d_prev = d
            return d_prev, total

        zero = jnp.zeros((chans, tokens), F32)
        lax.fori_loop(0, SWEEPS * groups, body, (zero, zero))
        if b == 0:
            pl.semaphore_wait(pltpu.get_barrier_semaphore(), n - 1)

        @pl.loop(1, n)
        def _(i):
            copy(b, i).start()

        out_ref[:, me * share + b] = res_scr[pl.ds(me * per, per), b]

    for b in range(share):
        @pl.loop(1, n)
        def _(i):
            copy(b, i).wait()


def solution(mesh):
    n = mesh.shape["time"]
    vmem = pl.BlockSpec(memory_space=pltpu.VMEM)
    smem = pl.BlockSpec(memory_space=pltpu.SMEM)

    def local(x_init, w_in, w_out, mod_scale, mod_shift, step_size):
        batch, tokens, chans = x_init.shape
        per, hidden = mod_scale.shape
        share = batch // n
        me = lax.axis_index("time")
        x_mine = lax.dynamic_slice_in_dim(jnp.swapaxes(x_init, 1, 2), me * share, share, 0)
        mods_t, steps, flag = pl.pallas_call(
            functools.partial(gather_kernel, n),
            out_shape=(
                jax.ShapeDtypeStruct((hidden, LANES), BF16),
                jax.ShapeDtypeStruct((n, 1, LANES), F32),
                jax.ShapeDtypeStruct((1,), jnp.int32),
            ),
            in_specs=[vmem, vmem, smem, vmem],
            out_specs=(vmem, vmem, smem),
            scratch_shapes=[
                pltpu.VMEM((2 * per, hidden), BF16),
                pltpu.VMEM((1, LANES), F32),
                pltpu.VMEM((n, 2 * per, hidden), BF16),
                pltpu.SemaphoreType.DMA((2, n)),
                pltpu.SemaphoreType.DMA((2, n)),
            ],
            compiler_params=pltpu.CompilerParams(collective_id=0, has_side_effects=True),
            name="gather",
        )(mod_scale, mod_shift, step_size, w_in)

        def sweeps(fold, *operands):
            return pl.pallas_call(
                functools.partial(sweeps_kernel, n, per, fold),
                out_shape=jax.ShapeDtypeStruct((per, batch, chans, tokens), F32),
                in_specs=[vmem] * 4 + [smem],
                out_specs=vmem,
                scratch_shapes=[
                    pltpu.VMEM((n * per if fold else 1, hidden, LANES), BF16),
                    pltpu.VMEM((n * per, chans, tokens), BF16),
                    pltpu.VMEM((n * per, share, chans, tokens), F32),
                    pltpu.SemaphoreType.DMA((share, n)),
                    pltpu.SemaphoreType.DMA((share, n)),
                ],
                compiler_params=pltpu.CompilerParams(
                    collective_id=1 if fold else 2, has_side_effects=True, vmem_limit_bytes=40 * 1024 * 1024),
                name="sweeps" if fold else "sweeps_wide",
            )(*operands)

        out = lax.cond(
            flag[0] != 0, functools.partial(sweeps, True), functools.partial(sweeps, False),
            x_mine, mods_t, w_in, w_out.T, steps)
        return jnp.swapaxes(out, 2, 3)

    return jax.shard_map(local, mesh=mesh, in_specs=(P("data"), P(), P(), P("time"), P("time"), P("time")), out_specs=P("time", "data"), check_vma=False)
```

time: 669 us -> 118 us (0.18)
  the two profiles are of different devices: /device:TPU:102 before, /device:TPU:97 now
where the time goes in v2:
time: 118 us
  Pallas kernels  114 us (97%)
  local copies, waits for them, and re-layouts  2.55 us (2%)
    pallas_call x1, Pallas kernels, sweeps(): pl.pallas_call(functools.partial(sweeps_kernel, n, per, fold), out_shape=...  98.3 us
    pallas_call x1, Pallas kernels, local(): pl.pallas_call(functools.partial(gather_kernel, n), out_shape=(jax.ShapeD...  16.1 us
    unnamed x3, local copies, waits for them, and re-layouts  2.55 us

profile of v2, /device:TPU:97, one launch (start us, length us, event | category | flops | bytes accessed | tf_op | source)
XLA Modules:
  0.0 117.6 jit_solution(14021220792726547933)
XLA Ops:
  0.0 0.0 copy-start
  0.0 1.2 %copy-done = f32[64,256,16]{1,2,0:T(8,128)S(1)} copy-done((f32[64,256,16]{1,2,0:T(8,128)S(1)}, f32[64,256,16]{1,2,0:T(8,128)}, u32[]{:S(2)}) %copy-start) | copy-done | bytes 1048600
  1.2 16.1 %gather.1 = (bf16[384,128]{1,0:T(8,128)(2,1)S(1)}, f32[32,1,128]{2,1,0:T(1,128)S(1)}, s32[1]{0:T(128)}) custom-call(bf16[2,384]{1,0:T(2,128)(2,1)} %scale_ref.1, bf16[2,384]{1,0:T(2,128)(2,1)} %shift_ref.1, f32[2]{0:T(128)} %step_ref.1, bf16[16,384]{1,0:T(8,128)(2,1)} %w_in_ref.1), custom_call_target="tpu_custom_call" | custom-call | tf_op jit(solution)/shard_map/gather/pallas_call | solution.py:202
  18.0 98.3 %conditional.1 = (f32[2,64,16,256]{3,2,1,0:T(8,128)S(1)}) conditional(s32[]{:T(128)} %bitcast, (f32[2,16,256]{2,1,0:T(8,128)S(1)}, bf16[384,128]{1,0:T(8,128)(2,1)S(1)}, bf16[16,384]{1,0:T(8,128)(2,1)}, bf16[16,384]{1,0:T(8,128)(2,1)}, f32[32,1,128]{2,1,0:T(1,128)S(1)}) %tuple.14, (f32[2,16,256]{2,1,0:T(8,128)S(1)}, bf16[384,128]{1,0:T(8,128)(2,1)S(1)}, ...), branch_computations={%region_0.0_spmd, %region_1.0_spmd} | conditional | bytes 8 | solution.py:240
  18.0 98.3 %sweeps.1 = f32[2,64,16,256]{3,2,1,0:T(8,128)S(1)} custom-call(f32[2,16,256]{2,1,0:T(8,128)S(1)} %get-tuple-element.33.x_ref, bf16[384,128]{1,0:T(8,128)(2,1)S(1)} %get-tuple-element.34.mods_t_ref, bf16[16,384]{1,0:T(8,128)(2,1)} %get-tuple-element.35.w_in_ref, bf16[16,384]{1,0:T(8,128)(2,1)} %get-tuple-element.36.w_out_ref, ...), custom_call_target="tpu_custom_call" | custom-call | tf_op jit(solution)/shard_map/cond/branch_1_fun/sweeps/pallas_call | solution.py:223
  116.3 1.3 %copy.10 = f32[2,64,256,16]{2,3,1,0:T(8,128)} copy(f32[2,64,256,16]{2,3,1,0:T(8,128)S(1)} %bitcast.5) | data formatting | bytes 4194304
  (1 shorter events, 0.0 us)
Async XLA Ops:
  0.0 1.2 %copy-start = (f32[64,256,16]{1,2,0:T(8,128)S(1)}, f32[64,256,16]{1,2,0:T(8,128)}, u32[]{:S(2)}) copy-start(f32[64,256,16]{1,2,0:T(8,128)} %param.8) | copy-start | bytes 3145732

commit v3 on v2

--- a/solution.py
+++ b/solution.py
@@ -10,6 +10,8 @@
 
 SWEEPS = 4
 UNROLL = 16
+PICKS = 4
+EARLY = 9
 AHEAD = 2
 LANES = 128
 FOLD_LIMIT = 2.0 ** 60
@@ -81,54 +83,72 @@
     return j // per * (2 * per) + lax.rem(j, per)
 
 
-def sweeps_kernel(n, per, fold, x_ref, mods_t_ref, w_in_ref, w_out_ref, step_ref, out_ref, w_scr, xs_scr, res_scr, send_sem, recv_sem):
+def sweeps_kernel(n, per, fold, x_hbm, mods_t_ref, w_in_ref, w_out_ref, step_ref, out_ref, x_scr, w_scr, xs_scr, z_scr, h_scr, res_scr, x_sem, send_sem, recv_sem):
     me = lax.axis_index("time")
     signal_all(n, me)
-    share, chans, tokens = x_ref.shape
+    share, chans, tokens = x_scr.shape
     steps = n * per
+    half_lanes = LANES // 2
+    load_x = pltpu.make_async_copy(x_hbm.at[pl.ds(me * share, share)], x_scr, x_sem)
+    load_x.start()
     mods_t = mods_t_ref[...]
 
     row = lax.broadcasted_iota(jnp.int32, (LANES, LANES), 0)
-    lane = lax.broadcasted_iota(jnp.int32, (LANES, LANES), 1)
-    lane_row = lax.broadcasted_iota(jnp.int32, (1, LANES), 1)
-    spread = one_hot((lane % chans == row) & (lane < 3 * chans))
+    lane = lax.broadcasted_iota(jnp.int32, (1, LANES), 1)
+    slot = lax.rem(lane, half_lanes)
+    spread = one_hot((lax.rem(lane, chans) == row) & (slot < 3 * chans))
     w3 = 0.5 * lax.dot_general(w_in_ref[...], spread[:chans], CONTRACT0, preferred_element_type=F32)
 
     if fold:
-        w3 = w3 + jnp.where(lane_row == 3 * chans, 0.5, 0.0)
-        ones = jnp.where(lane_row < 3 * chans, 1.0, 0.0)
-        use_hi = (lane_row < chans) | (lane_row >= 3 * chans)
-        use_mid = lane_row < 2 * chans
-
-        @pl.loop(0, steps)
-        def _(j):
-            src = scale_row(j, per)
-            pick = ((row == src) & (lane < 3 * chans)) | ((row == src + per) & (lane == 3 * chans))
-            picked = jnp.dot(mods_t, one_hot(pick), preferred_element_type=F32)
-            prod = w3 * (picked + ones)
-            hi = prod.astype(BF16).astype(F32)
-            rest = prod - hi
-            mid = rest.astype(BF16).astype(F32)
-            w_scr[j] = jnp.where(use_hi, hi, jnp.where(use_mid, mid, rest - mid)).astype(BF16)
+        w3 = w3 + jnp.where(slot == 3 * chans, 0.5, 0.0)
+        ones = jnp.where(slot < 3 * chans, 1.0, 0.0)
+        rest_lanes = (slot >= chans) & (slot < 3 * chans)
+        low_lanes = (slot >= 2 * chans) & (slot < 3 * chans)
+        wide_row = lax.broadcasted_iota(jnp.int32, (LANES, 2 * LANES), 0)
+        wide_lane = lax.broadcasted_iota(jnp.int32, (1, 2 * LANES), 1)
+        wide_slot = lax.rem(wide_lane, half_lanes)
+        source = scale_row(wide_lane // half_lanes, per) + jnp.where(wide_slot == 3 * chans, per, 0)
+        source = jnp.where(wide_slot <= 3 * chans, source, -8 * steps)
+        ahead = wide_row - source
+
+        def build(g, unused):
+            picked = []
+            for t in range(PICKS):
+                first = (g * PICKS + t) * 8
+                picked.append(jnp.dot(mods_t, one_hot(ahead == first), preferred_element_type=F32))
+            for t in range(PICKS):
+                for p in range(2):
+                    prod = w3 * (picked[t][:, p * LANES:(p + 1) * LANES] + ones)
+                    rest = prod - jnp.where(rest_lanes, prod.astype(BF16).astype(F32), 0.0)
+                    rest = rest - jnp.where(low_lanes, rest.astype(BF16).astype(F32), 0.0)
+                    w_scr[(g * PICKS + t) * 2 + p] = rest.astype(BF16)
+            return unused
+
+        lax.fori_loop(0, steps // (4 * PICKS), build, 0)
     else:
-        w_scr[0] = (w3 * jnp.where(lane_row < chans, 2.0, 0.0)).astype(BF16)
+        w_scr[0] = (w3 * jnp.where(lane < chans, 2.0, 0.0)).astype(BF16)
 
     w_out_t = w_out_ref[...]
     ones_rows = jnp.ones((chans, tokens), BF16)
-    zero_rows = jnp.zeros((LANES - 4 * chans, tokens), BF16)
+    zero_rows = jnp.zeros((half_lanes, tokens), BF16)
     row_tok = lax.broadcasted_iota(jnp.int32, (LANES, tokens), 0)
-    unroll = UNROLL if fold else per
+    unroll = UNROLL if fold else 2 * AHEAD
     groups = steps // unroll
-
-    def half_pre(j, x):
-        rhs = jnp.concatenate([x, x, x, ones_rows, zero_rows], axis=0)
+    early = max(unroll - EARLY, 0)
+
+    def half_pre(j0, u, x):
+        parts = [x, x, x, ones_rows]
         if fold:
-            return jnp.dot(w_scr[j], rhs, preferred_element_type=F32)
-        u = jnp.dot(w_scr[0], rhs, preferred_element_type=F32)
-        src = scale_row(j, per)
+            rhs = jnp.concatenate(parts + [zero_rows] if u % 2 == 0 else [zero_rows] + parts, axis=0)
+            return jnp.dot(w_scr[j0 // 2 + u // 2], rhs, preferred_element_type=F32)
+        pre = jnp.dot(w_scr[0], jnp.concatenate(parts + [zero_rows], axis=0), preferred_element_type=F32)
+        src = scale_row(j0 + u, per)
         scale = jnp.dot(mods_t, one_hot(row_tok == src), preferred_element_type=F32)
         shift = jnp.dot(mods_t, one_hot(row_tok == src + per), preferred_element_type=F32)
-        return 0.5 * (u * (1.0 + scale) + shift)
+        return 0.5 * (pre * (1.0 + scale) + shift)
+
+    def project(hidden):
+        return jnp.dot(w_out_t, hidden, preferred_element_type=F32)
 
     def copy(b, i):
         q = lax.rem(me + i, n)
@@ -136,43 +156,55 @@
             res_scr.at[pl.ds(q * per, per), b], out_ref.at[:, me * share + b], send_sem.at[b, i], recv_sem.at[b, i],
             device_id={"time": q}, device_id_type=MESH)
 
+    load_x.wait()
     for b in range(share):
-        x0 = x_ref[b]
+        x0 = x_scr[b]
         x0_bf = x0.astype(BF16)
 
         @pl.loop(0, steps)
         def _(j):
             xs_scr[j] = x0_bf
 
+        def advance(j, d, d_prev, total, first=None):
+            i = jnp.maximum(j - 1, 0)
+            total = total + step_ref[i // per, 0, lax.rem(i, per)] * (0.5 * (d_prev + d))
+            if first is not None:
+                total = jnp.where(first, 0.0, total)
+            new = x0 + total
+            xs_scr[j] = new.astype(BF16)
+            res_scr[j, b] = new
+            return d, total
+
         def body(g, carry):
-            d_prev, total = carry
             j0 = lax.rem(g, groups) * unroll
-            xs = [xs_scr[j0 + u] for u in range(unroll)]
-            halves, ds = {}, []
-            for u in range(unroll + AHEAD):
-                if u < unroll:
-                    halves[u] = half_pre(j0 + u, xs[u])
-                if u >= AHEAD:
-                    half = halves.pop(u - AHEAD)
-                    arg = half * (half * half * C3 + C1)
-                    hidden = (half * (1.0 + jnp.tanh(arg))).astype(BF16)
-                    ds.append(jnp.dot(w_out_t, hidden, preferred_element_type=F32))
+            j_next = lax.rem(g + 1, groups) * unroll
+            xs = [xs_scr[j0 + u] for u in range(AHEAD, unroll)] + [xs_scr[j_next + u] for u in range(AHEAD)]
+            ds = [project(h_scr[...])]
+            halves = {u: z_scr[u] for u in range(AHEAD)}
             for u in range(unroll):
-                j = j0 + u
-                d = ds[u]
-                i = jnp.maximum(j - 1, 0)
-                inc = step_ref[i // per, 0, lax.rem(i, per)] * (0.5 * (d_prev + d))
-                total = total + inc
-                if u == 0:
-                    total = jnp.where(j0 == 0, 0.0, total)
-                new = x0 + total
-                xs_scr[j] = new.astype(BF16)
-                res_scr[j, b] = new
-                d_prev = d
-            return d_prev, total
-
+                v = u + AHEAD
+                if v < unroll:
+                    halves[v] = half_pre(j0, v, xs[u])
+                half = halves.pop(u)
+                arg = half * (half * half * C3 + C1)
+                hidden = (half * (1.0 + jnp.tanh(arg))).astype(BF16)
+                if early <= u < early + AHEAD:
+                    z_scr[u - early] = half_pre(j_next, u - early, xs[u - early - AHEAD])
+                if u < unroll - 1:
+                    ds.append(project(hidden))
+                else:
+                    h_scr[...] = hidden
+            carry = advance(lax.rem(j0 + steps - 1, steps), ds[0], *carry)
+            for u in range(unroll - 1):
+                carry = advance(j0 + u, ds[u + 1], *carry, first=j0 == 0 if u == 0 else None)
+            return carry
+
+        for u in range(AHEAD):
+            z_scr[u] = half_pre(0, u, x0_bf)
+        h_scr[...] = jnp.zeros_like(h_scr)
         zero = jnp.zeros((chans, tokens), F32)
-        lax.fori_loop(0, SWEEPS * groups, body, (zero, zero))
+        carry = lax.fori_loop(0, SWEEPS * groups, body, (zero, zero))
+        advance(steps - 1, project(h_scr[...]), *carry)
         if b == 0:
             pl.semaphore_wait(pltpu.get_barrier_semaphore(), n - 1)
 
@@ -197,8 +229,6 @@
         batch, tokens, chans = x_init.shape
         per, hidden = mod_scale.shape
         share = batch // n
-        me = lax.axis_index("time")
-        x_mine = lax.dynamic_slice_in_dim(jnp.swapaxes(x_init, 1, 2), me * share, share, 0)
         mods_t, steps, flag = pl.pallas_call(
             functools.partial(gather_kernel, n),
             out_shape=(
@@ -223,12 +253,16 @@
             return pl.pallas_call(
                 functools.partial(sweeps_kernel, n, per, fold),
                 out_shape=jax.ShapeDtypeStruct((per, batch, chans, tokens), F32),
-                in_specs=[vmem] * 4 + [smem],
+                in_specs=[pl.BlockSpec(memory_space=pl.ANY)] + [vmem] * 3 + [smem],
                 out_specs=vmem,
                 scratch_shapes=[
-                    pltpu.VMEM((n * per if fold else 1, hidden, LANES), BF16),
+                    pltpu.VMEM((share, chans, tokens), F32),
+                    pltpu.VMEM((n * per // 2 if fold else 1, hidden, LANES), BF16),
                     pltpu.VMEM((n * per, chans, tokens), BF16),
+                    pltpu.VMEM((AHEAD, hidden, tokens), F32),
+                    pltpu.VMEM((hidden, tokens), BF16),
                     pltpu.VMEM((n * per, share, chans, tokens), F32),
+                    pltpu.SemaphoreType.DMA,
                     pltpu.SemaphoreType.DMA((share, n)),
                     pltpu.SemaphoreType.DMA((share, n)),
                 ],
@@ -239,7 +273,7 @@
 
         out = lax.cond(
             flag[0] != 0, functools.partial(sweeps, True), functools.partial(sweeps, False),
-            x_mine, mods_t, w_in, w_out.T, steps)
+            jnp.swapaxes(x_init, 1, 2), mods_t, w_in, w_out.T, steps)
         return jnp.swapaxes(out, 2, 3)
 
     return jax.shard_map(local, mesh=mesh, in_specs=(P("data"), P(), P(), P("time"), P("time"), P("time")), out_specs=P("time", "data"), check_vma=False)

time: 118 us -> 97.6 us (0.83)
  Pallas kernels: 114 us -> 95.3 us
  local copies, waits for them, and re-layouts: 2.55 us -> 1.32 us
    pallas_call x1, Pallas kernels: 98.3 us -> 79.2 us  [sweeps(): pl.pallas_call(functools.partial(sweeps_kernel, n, per, fold), out_shape=...]
    unnamed x3 -> x1, local copies, waits for them, and re-layouts: 2.55 us -> 1.32 us
where the time goes in v3:
time: 97.6 us; the launch traced here: 97.3 us
  Pallas kernels  95.3 us (98%)
  local copies, waits for them, and re-layouts  1.32 us (1%)
    pallas_call x1, Pallas kernels, sweeps(): pl.pallas_call(functools.partial(sweeps_kernel, n, per, fold), out_shape=...  79.2 us
    pallas_call x1, Pallas kernels, local(): pl.pallas_call(functools.partial(gather_kernel, n), out_shape=(jax.ShapeD...  16.1 us

profile of v3, /device:TPU:97, one launch (start us, length us, event | category | flops | bytes accessed | tf_op | source)
XLA Modules:
  0.0 97.3 jit_solution(7814414059721130580)
XLA Ops:
  0.0 16.1 %gather.1 = (bf16[384,128]{1,0:T(8,128)(2,1)S(1)}, f32[32,1,128]{2,1,0:T(1,128)S(1)}, s32[1]{0:T(128)}) custom-call(bf16[2,384]{1,0:T(2,128)(2,1)} %scale_ref.1, bf16[2,384]{1,0:T(2,128)(2,1)} %shift_ref.1, f32[2]{0:T(128)} %step_ref.1, bf16[16,384]{1,0:T(8,128)(2,1)} %w_in_ref.1), custom_call_target="tpu_custom_call" | custom-call | tf_op jit(solution)/shard_map/gather/pallas_call | solution.py:232
  16.7 79.2 %conditional.1 = (f32[2,64,16,256]{3,2,1,0:T(8,128)S(1)}) conditional(s32[]{:T(128)} %bitcast, (f32[64,16,256]{2,1,0:T(8,128)}, bf16[384,128]{1,0:T(8,128)(2,1)S(1)}, bf16[16,384]{1,0:T(8,128)(2,1)}, bf16[16,384]{1,0:T(8,128)(2,1)}, f32[32,1,128]{2,1,0:T(1,128)S(1)}) %tuple.16, (f32[64,16,256]{2,1,0:T(8,128)}, bf16[384,128]{1,0:T(8,128)(2,1)S(1)}, ...), branch_computations={%region_0.0_spmd, %region_1.0_spmd} | conditional | bytes 8 | solution.py:274
  16.7 79.2 %sweeps.1 = f32[2,64,16,256]{3,2,1,0:T(8,128)S(1)} custom-call(f32[64,16,256]{2,1,0:T(8,128)} %get-tuple-element.33.x_hbm, bf16[384,128]{1,0:T(8,128)(2,1)S(1)} %get-tuple-element.34.mods_t_ref, bf16[16,384]{1,0:T(8,128)(2,1)} %get-tuple-element.35.w_in_ref, bf16[16,384]{1,0:T(8,128)(2,1)} %get-tuple-element.36.w_out_ref, ...), custom_call_target="tpu_custom_call" | custom-call | tf_op jit(solution)/shard_map/cond/branch_1_fun/sweeps/pallas_call | solution.py:253
  95.9 1.3 %copy.10 = f32[2,64,256,16]{2,3,1,0:T(8,128)} copy(f32[2,64,256,16]{2,3,1,0:T(8,128)S(1)} %bitcast.4) | data formatting | bytes 4194304

commit v4 on v3

v4 whole, which is shorter than its diff:
```python
import functools
import math

import jax
import jax.numpy as jnp
from jax import lax
from jax.experimental import pallas as pl
from jax.experimental.pallas import tpu as pltpu
from jax.sharding import PartitionSpec as P

SWEEPS = 4
UNROLL = 16
PICKS = 4
EARLY = 9
AHEAD = 2
LANES = 128
WIDTH = 128
FOLD_LIMIT = 2.0 ** 60
C1 = 2.0 * math.sqrt(2.0 / math.pi)
C3 = 8.0 * math.sqrt(2.0 / math.pi) * 0.044715
F32, BF16 = jnp.float32, jnp.bfloat16
MESH = pl.DeviceIdType.MESH
CONTRACT0 = (((0,), (0,)), ((), ()))


def offsets(n):
    return sorted(range(1, n), key=lambda i: (abs(2 * i - n), i))


def signal_all(n, me):
    barrier = pltpu.get_barrier_semaphore()
    for i in offsets(n):
        pl.semaphore_signal(barrier, inc=1, device_id={"time": lax.rem(me + i, n)}, device_id_type=MESH)


def wait_bytes(ref, *sems):
    for sem in sems:
        pltpu.make_async_copy(ref, ref, sem).wait()


def one_hot(cond):
    return jnp.where(cond, 1.0, 0.0).astype(BF16)


def gather_kernel(n, scale_hbm, shift_hbm, step_hbm, w_in_hbm, mods_t_ref, steps_ref, flag_ref, scale, shift, step, w_in, mine, mine_step, mods, load_sem, send_sem, recv_sem):
    me = lax.axis_index("time")
    loads = [
        pltpu.make_async_copy(src, dst, load_sem.at[k])
        for k, (src, dst) in enumerate(((scale_hbm, scale), (shift_hbm, shift), (step_hbm, step), (w_in_hbm, w_in)))
    ]
    for load in loads:
        load.start()
    signal_all(n, me)
    for load in loads:
        load.wait()
    per = scale.shape[0]
    mine[0:per] = scale[...]
    mine[per:2 * per] = shift[...]
    lane = lax.broadcasted_iota(jnp.int32, (1, LANES), 1)
    row = jnp.zeros((1, LANES), F32)
    for i in range(per):
        row = jnp.where(lane == i, step[i], row)
    mine_step[...] = row
    mods[me] = mine[...]
    steps_ref[me] = mine_step[...]
    w_top = jnp.max(jnp.abs(w_in[...].astype(F32)))
    pl.semaphore_wait(pltpu.get_barrier_semaphore(), n - 1)

    for i in offsets(n):
        to = {"time": lax.rem(me + i, n)}
        pltpu.make_async_remote_copy(mine, mods.at[me], send_sem.at[0], recv_sem.at[0], device_id=to, device_id_type=MESH).start()
        pltpu.make_async_remote_copy(mine_step, steps_ref.at[me], send_sem.at[1], recv_sem.at[1], device_id=to, device_id_type=MESH).start()
    wait_bytes(mods.at[pl.ds(0, n - 1)], recv_sem.at[0])

    parts = [mods[q].astype(F32) for q in range(n)]
    flat = jnp.concatenate(parts, axis=0).astype(BF16)
    r = lax.broadcasted_iota(jnp.int32, (LANES, LANES), 0)
    c = lax.broadcasted_iota(jnp.int32, (LANES, LANES), 1)
    mods_t_ref[...] = lax.dot_general(flat, one_hot(r == c), CONTRACT0, preferred_element_type=F32).astype(BF16)
    top = 0.0
    for q in range(n):
        top = jnp.maximum(top, jnp.abs(1.0 + parts[q][:per]))
    flag_ref[0] = (jnp.max(top) * w_top <= FOLD_LIMIT).astype(jnp.int32)
    wait_bytes(steps_ref.at[pl.ds(0, n - 1)], recv_sem.at[1], send_sem.at[1])
    wait_bytes(mods.at[pl.ds(0, n - 1)], send_sem.at[0])


def scale_row(j, per):
    return j // per * (2 * per) + lax.rem(j, per)


def sweeps_kernel(n, per, fold, x_hbm, mods_t_ref, w_in_ref, w_out_ref, step_ref, out_ref, x_scr, w_scr, xs_scr, z_scr, h_scr, res_scr, x_sem, send_sem, recv_sem):
    me = lax.axis_index("time")
    chunks, chans, width = x_scr.shape
    tokens = x_hbm.shape[2]
    cuts = tokens // width
    share = chunks // cuts
    steps = n * per
    tiles = steps // 2
    half_lanes = LANES // 2

    def x_copy(c):
        return pltpu.make_async_copy(x_hbm.at[me * share + c // cuts, :, pl.ds(c % cuts * width, width)], x_scr.at[c], x_sem.at[c])

    for c in range(chunks):
        x_copy(c).start()
    signal_all(n, me)
    mods_t = mods_t_ref[...]

    row = lax.broadcasted_iota(jnp.int32, (LANES, LANES), 0)
    lane = lax.broadcasted_iota(jnp.int32, (1, LANES), 1)
    slot = lax.rem(lane, half_lanes)
    spread = one_hot((lax.rem(lane, chans) == row) & (slot < 3 * chans))
    w3 = 0.5 * lax.dot_general(w_in_ref[...], spread[:chans], CONTRACT0, preferred_element_type=F32)
    wide_row = lax.broadcasted_iota(jnp.int32, (LANES, 2 * LANES), 0)
    wide_lane = lax.broadcasted_iota(jnp.int32, (1, 2 * LANES), 1)

    if fold:
        w3 = w3 + jnp.where(slot == 3 * chans, 0.5, 0.0)
        ones = jnp.where(slot < 3 * chans, 1.0, 0.0)
        rest_lanes = (slot >= chans) & (slot < 3 * chans)
        low_lanes = (slot >= 2 * chans) & (slot < 3 * chans)
        wide_slot = lax.rem(wide_lane, half_lanes)
        source = scale_row(wide_lane // half_lanes, per) + jnp.where(wide_slot == 3 * chans, per, 0)
        source = jnp.where(wide_slot <= 3 * chans, source, -8 * steps)
        ahead = wide_row - source

        def build(g, unused):
            picked = []
            for t in range(PICKS):
                first = (g * PICKS + t) * 8
                picked.append(jnp.dot(mods_t, one_hot(ahead == first), preferred_element_type=F32))
            for t in range(PICKS):
                for p in range(2):
                    prod = w3 * (picked[t][:, p * LANES:(p + 1) * LANES] + ones)
                    rest = prod - jnp.where(rest_lanes, prod.astype(BF16).astype(F32), 0.0)
                    rest = rest - jnp.where(low_lanes, rest.astype(BF16).astype(F32), 0.0)
                    w_scr[(g * PICKS + t) * 2 + p] = rest.astype(BF16)
            return unused

        lax.fori_loop(0, steps // (4 * PICKS), build, 0)
    else:
        w_scr[0] = (w3 * jnp.where(lane < chans, 2.0, 0.0)).astype(BF16)

    w_out_t = w_out_ref[...]
    ones_rows = jnp.ones((chans, width), BF16)
    zero_rows = jnp.zeros((half_lanes, width), BF16)
    unroll = UNROLL if fold else 2 * AHEAD
    groups = tiles // unroll
    per_chunk = SWEEPS * groups
    early = max(unroll - EARLY, 0)

    def half_pre(t, x):
        tops = [jnp.concatenate([x[p], x[p], x[p], ones_rows], axis=0) for p in range(2)]
        if fold:
            left = jnp.concatenate([tops[0], zero_rows], axis=0)
            right = jnp.concatenate([zero_rows, tops[1]], axis=0)
            return jnp.dot(w_scr[t], jnp.concatenate([left, right], axis=1), preferred_element_type=F32)
        rhs = jnp.concatenate([jnp.concatenate([top, zero_rows], axis=0) for top in tops], axis=1)
        pre = jnp.dot(w_scr[0], rhs, preferred_element_type=F32)
        src = scale_row(2 * t + wide_lane // width, per)
        scale = jnp.dot(mods_t, one_hot(wide_row == src), preferred_element_type=F32)
        shift = jnp.dot(mods_t, one_hot(wide_row == src + per), preferred_element_type=F32)
        return 0.5 * (pre * (1.0 + scale) + shift)

    def project(hidden):
        return jnp.dot(w_out_t, hidden, preferred_element_type=F32)

    def load_xs(t):
        return xs_scr[2 * t], xs_scr[2 * t + 1]

    def advance(g, t, d, d_prev, total, first=None):
        c = jnp.maximum(g, 0) // per_chunk
        x0 = x_scr[c]
        x_next = x_scr[jnp.minimum((g + per_chunk) // per_chunk, chunks - 1)]
        last = lax.rem(g + per_chunk, per_chunk) >= per_chunk - groups
        for p in range(2):
            j = 2 * t + p
            i = jnp.maximum(j - 1, 0)
            part = d[:, p * width:(p + 1) * width]
            total = total + step_ref[i // per, 0, lax.rem(i, per)] * (0.5 * (d_prev + part))
            if p == 0 and first is not None:
                total = jnp.where(first, 0.0, total)
            new = x0 + total
            xs_scr[j] = jnp.where(last, x_next, new).astype(BF16)
            res_scr[j, c] = new
            d_prev = part
        return d_prev, total

    def send(c):
        place = (slice(None), me * share + c // cuts, slice(None), pl.ds(pl.multiple_of(lax.rem(c, cuts) * width, width), width))
        for i in offsets(n):
            q = lax.rem(me + i, n)
            pltpu.make_async_remote_copy(
                res_scr.at[pl.ds(q * per, per), c], out_ref.at[place], send_sem, recv_sem,
                device_id={"time": q}, device_id_type=MESH).start()
        out_ref[place] = res_scr[pl.ds(me * per, per), c]

    def body(g, carry):
        t0 = lax.rem(g, groups) * unroll
        t_next = lax.rem(g + 1, groups) * unroll
        xs = [load_xs(t0 + u) for u in range(AHEAD, unroll)] + [load_xs(t_next + u) for u in range(AHEAD)]
        ds = [project(h_scr[...])]
        halves = {u: z_scr[u] for u in range(AHEAD)}
        for u in range(unroll):
            v = u + AHEAD
            if v < unroll:
                halves[v] = half_pre(t0 + v, xs[u])
            half = halves.pop(u)
            arg = half * (half * half * C3 + C1)
            hidden = (half * (1.0 + jnp.tanh(arg))).astype(BF16)
            if early <= u < early + AHEAD:
                z_scr[u - early] = half_pre(t_next + u - early, xs[u - early - AHEAD])
            if u < unroll - 1:
                ds.append(project(hidden))
            else:
                h_scr[...] = hidden
        carry = advance(g - 1, lax.rem(t0 + tiles - 1, tiles), ds[0], *carry)
        for u in range(unroll - 1):
            carry = advance(g, t0 + u, ds[u + 1], *carry, first=t0 == 0 if u == 0 else None)

        @pl.when((g > 0) & (lax.rem(g, per_chunk) == 0))
        def _():
            send(g // per_chunk - 1)

        return carry

    for c in range(chunks):
        x_copy(c).wait()
    x_first = x_scr[0].astype(BF16)

    @pl.loop(0, steps)
    def _(j):
        xs_scr[j] = x_first

    for u in range(AHEAD):
        z_scr[u] = half_pre(u, (x_first, x_first))
    h_scr[...] = jnp.zeros_like(h_scr)
    pl.semaphore_wait(pltpu.get_barrier_semaphore(), n - 1)
    zero = jnp.zeros((chans, width), F32)
    total_groups = chunks * per_chunk
    carry = lax.fori_loop(0, total_groups, body, (zero, zero))
    advance(total_groups - 1, tiles - 1, project(h_scr[...]), *carry)
    send(chunks - 1)
    wait_bytes(res_scr.at[pl.ds(0, (n - 1) * per)], recv_sem, send_sem)


def solution(mesh):
    n = mesh.shape["time"]
    vmem = pl.BlockSpec(memory_space=pltpu.VMEM)
    smem = pl.BlockSpec(memory_space=pltpu.SMEM)

    def local(x_init, w_in, w_out, mod_scale, mod_shift, step_size):
        batch, tokens, chans = x_init.shape
        per, hidden = mod_scale.shape
        share = batch // n
        any_spec = pl.BlockSpec(memory_space=pl.ANY)
        mods_t, steps, flag = pl.pallas_call(
            functools.partial(gather_kernel, n),
            out_shape=(
                jax.ShapeDtypeStruct((hidden, LANES), BF16),
                jax.ShapeDtypeStruct((n, 1, LANES), F32),
                jax.ShapeDtypeStruct((1,), jnp.int32),
            ),
            in_specs=[any_spec] * 4,
            out_specs=(vmem, vmem, smem),
            scratch_shapes=[
                pltpu.VMEM((per, hidden), BF16),
                pltpu.VMEM((per, hidden), BF16),
                pltpu.SMEM((per,), F32),
                pltpu.VMEM((chans, hidden), BF16),
                pltpu.VMEM((2 * per, hidden), BF16),
                pltpu.VMEM((1, LANES), F32),
                pltpu.VMEM((n, 2 * per, hidden), BF16),
                pltpu.SemaphoreType.DMA((4,)),
                pltpu.SemaphoreType.DMA((2,)),
                pltpu.SemaphoreType.DMA((2,)),
            ],
            compiler_params=pltpu.CompilerParams(collective_id=0, has_side_effects=True),
            name="gather",
        )(mod_scale, mod_shift, step_size, w_in)

        def sweeps(fold, *operands):
            chunks = share * tokens // WIDTH
            return pl.pallas_call(
                functools.partial(sweeps_kernel, n, per, fold),
                out_shape=jax.ShapeDtypeStruct((per, batch, chans, tokens), F32),
                in_specs=[any_spec] + [vmem] * 3 + [smem],
                out_specs=vmem,
                scratch_shapes=[
                    pltpu.VMEM((chunks, chans, WIDTH), F32),
                    pltpu.VMEM((n * per // 2 if fold else 1, hidden, LANES), BF16),
                    pltpu.VMEM((n * per, chans, WIDTH), BF16),
                    pltpu.VMEM((AHEAD, hidden, 2 * WIDTH), F32),
                    pltpu.VMEM((hidden, 2 * WIDTH), BF16),
                    pltpu.VMEM((n * per, chunks, chans, WIDTH), F32),
                    pltpu.SemaphoreType.DMA((chunks,)),
                    pltpu.SemaphoreType.DMA,
                    pltpu.SemaphoreType.DMA,
                ],
                compiler_params=pltpu.CompilerParams(
                    collective_id=1 if fold else 2, has_side_effects=True, vmem_limit_bytes=40 * 1024 * 1024),
                name="sweeps" if fold else "sweeps_wide",
            )(*operands)

        out = lax.cond(
            flag[0] != 0, functools.partial(sweeps, True), functools.partial(sweeps, False),
            jnp.swapaxes(x_init, 1, 2), mods_t, w_in, w_out.T, steps)
        return jnp.swapaxes(out, 2, 3)

    return jax.shard_map(local, mesh=mesh, in_specs=(P("data"), P(), P(), P("time"), P("time"), P("time")), out_specs=P("time", "data"), check_vma=False)
```

time: 97.6 us -> 87.9 us (0.901)
  Pallas kernels: 95.3 us -> 85.6 us
    pallas_call x1, Pallas kernels: 79.2 us -> 72.3 us  [sweeps(): pl.pallas_call(functools.partial(sweeps_kernel, n, per, fold), out_shape=...]
    pallas_call x1, Pallas kernels: 16.1 us -> 13.3 us  [local(): pl.pallas_call(functools.partial(gather_kernel, n), out_shape=(jax.ShapeD...]
where the time goes in v4:
time: 87.9 us; the launch traced here: 87.6 us
  Pallas kernels  85.6 us (97%)
  local copies, waits for them, and re-layouts  1.32 us (2%)
    pallas_call x1, Pallas kernels, sweeps(): pl.pallas_call(functools.partial(sweeps_kernel, n, per, fold), out_shape=...  72.3 us
    pallas_call x1, Pallas kernels, local(): pl.pallas_call(functools.partial(gather_kernel, n), out_shape=(jax.ShapeD...  13.3 us

profile of v4, /device:TPU:97, one launch (start us, length us, event | category | flops | bytes accessed | tf_op | source)
XLA Modules:
  0.0 87.6 jit_solution(18164520672274785010)
XLA Ops:
  0.0 13.3 %gather.1 = (bf16[384,128]{1,0:T(8,128)(2,1)S(1)}, f32[32,1,128]{2,1,0:T(1,128)S(1)}, s32[1]{0:T(128)}) custom-call(bf16[2,384]{1,0:T(2,128)(2,1)} %scale_hbm.1, bf16[2,384]{1,0:T(2,128)(2,1)} %shift_hbm.1, f32[2]{0:T(128)} %step_hbm.1, bf16[16,384]{1,0:T(8,128)(2,1)} %w_in_hbm.1), custom_call_target="tpu_custom_call" | custom-call | tf_op jit(solution)/shard_map/gather/pallas_call | solution.py:258
  14.0 72.3 %conditional.1 = (f32[2,64,16,256]{3,2,1,0:T(8,128)S(1)}) conditional(s32[]{:T(128)} %bitcast, (f32[64,16,256]{2,1,0:T(8,128)}, bf16[384,128]{1,0:T(8,128)(2,1)S(1)}, bf16[16,384]{1,0:T(8,128)(2,1)}, bf16[16,384]{1,0:T(8,128)(2,1)}, f32[32,1,128]{2,1,0:T(1,128)S(1)}) %tuple.16, (f32[64,16,256]{2,1,0:T(8,128)}, bf16[384,128]{1,0:T(8,128)(2,1)S(1)}, ...), branch_computations={%region_0.0_spmd, %region_1.0_spmd} | conditional | bytes 8 | solution.py:306
  14.0 72.3 %sweeps.1 = f32[2,64,16,256]{3,2,1,0:T(8,128)S(1)} custom-call(f32[64,16,256]{2,1,0:T(8,128)} %get-tuple-element.33.x_hbm, bf16[384,128]{1,0:T(8,128)(2,1)S(1)} %get-tuple-element.34.mods_t_ref, bf16[16,384]{1,0:T(8,128)(2,1)} %get-tuple-element.35.w_in_ref, bf16[16,384]{1,0:T(8,128)(2,1)} %get-tuple-element.36.w_out_ref, ...), custom_call_target="tpu_custom_call" | custom-call | tf_op jit(solution)/shard_map/cond/branch_1_fun/sweeps/pallas_call | solution.py:285
  86.3 1.3 %copy.10 = f32[2,64,256,16]{2,3,1,0:T(8,128)} copy(f32[2,64,256,16]{2,3,1,0:T(8,128)S(1)} %bitcast.4) | data formatting | bytes 4194304

commit v5 on v4

v5 whole, which is shorter than its diff:
```python
import functools
import math

import jax
import jax.numpy as jnp
from jax import lax
from jax.experimental import pallas as pl
from jax.experimental.pallas import tpu as pltpu
from jax.sharding import PartitionSpec as P

SWEEPS = 4
UNROLL = 16
PICKS = 4
EARLY = 9
AHEAD = 2
LANES = 128
WIDTH = 128
FOLD_LIMIT = 2.0 ** 60
C1 = 2.0 * math.sqrt(2.0 / math.pi)
C3 = 8.0 * math.sqrt(2.0 / math.pi) * 0.044715
F32, BF16 = jnp.float32, jnp.bfloat16
MESH = pl.DeviceIdType.MESH
CONTRACT0 = (((0,), (0,)), ((), ()))


def offsets(n):
    return sorted(range(1, n), key=lambda i: (abs(2 * i - n), i))


def signal_all(n, me):
    barrier = pltpu.get_barrier_semaphore()
    for i in offsets(n):
        pl.semaphore_signal(barrier, inc=1, device_id={"time": lax.rem(me + i, n)}, device_id_type=MESH)


def wait_bytes(ref, *sems):
    for sem in sems:
        pltpu.make_async_copy(ref, ref, sem).wait()


def one_hot(cond):
    return jnp.where(cond, 1.0, 0.0).astype(BF16)


def share_parameters(n, me, scale, shift, step, mine, mine_step, mods, steps, send_sem, recv_sem):
    per = scale.shape[0]
    mine[0:per] = scale[...]
    mine[per:2 * per] = shift[...]
    lane = lax.broadcasted_iota(jnp.int32, (1, LANES), 1)
    row = jnp.zeros((1, LANES), F32)
    for i in range(per):
        row = jnp.where(lane == i, step[i], row)
    mine_step[...] = row
    mods[me] = mine[...]
    steps[me] = mine_step[...]
    pl.semaphore_wait(pltpu.get_barrier_semaphore(), n - 1)
    for k, (src, dst) in enumerate(((mine, mods), (mine_step, steps))):
        for i in offsets(n):
            pltpu.make_async_remote_copy(
                src, dst.at[me], send_sem.at[k], recv_sem.at[k],
                device_id={"time": lax.rem(me + i, n)}, device_id_type=MESH).start()


def fold_is_safe(parts, per, w_in):
    top = 0.0
    for part in parts:
        top = jnp.maximum(top, jnp.abs(1.0 + part[:per]))
    return (jnp.max(top) * jnp.max(jnp.abs(w_in.astype(F32))) <= FOLD_LIMIT).astype(jnp.int32)


def scale_row(j, per):
    return j // per * (2 * per) + lax.rem(j, per)


def run_sweeps(n, per, fold, me, get_mods_t, w_in, w_out_t, ready, step_ref, out_ref, x_scr, w_scr, xs_scr, z_scr, h_scr, res_scr, send_sem, recv_sem):
    chunks, chans, width = x_scr.shape
    tokens = res_scr.shape[3]
    cuts = tokens // width
    share = chunks // cuts
    steps = n * per
    tiles = steps // 2
    half_lanes = LANES // 2

    row = lax.broadcasted_iota(jnp.int32, (LANES, LANES), 0)
    lane = lax.broadcasted_iota(jnp.int32, (1, LANES), 1)
    slot = lax.rem(lane, half_lanes)
    spread = one_hot((lax.rem(lane, chans) == row) & (slot < 3 * chans))
    w3 = 0.5 * lax.dot_general(w_in, spread[:chans], CONTRACT0, preferred_element_type=F32)
    wide_row = lax.broadcasted_iota(jnp.int32, (LANES, 2 * LANES), 0)
    wide_lane = lax.broadcasted_iota(jnp.int32, (1, 2 * LANES), 1)

    if fold:
        w3 = w3 + jnp.where(slot == 3 * chans, 0.5, 0.0)
        ones = jnp.where(slot < 3 * chans, 1.0, 0.0)
        rest_lanes = (slot >= chans) & (slot < 3 * chans)
        low_lanes = (slot >= 2 * chans) & (slot < 3 * chans)
        wide_slot = lax.rem(wide_lane, half_lanes)
        source = scale_row(wide_lane // half_lanes, per) + jnp.where(wide_slot == 3 * chans, per, 0)
        source = jnp.where(wide_slot <= 3 * chans, source, -8 * steps)
        ahead = wide_row - source
        mods_t = get_mods_t()

        def build(g, unused):
            picked = []
            for t in range(PICKS):
                first = (g * PICKS + t) * 8
                picked.append(jnp.dot(mods_t, one_hot(ahead == first), preferred_element_type=F32))
            for t in range(PICKS):
                for p in range(2):
                    prod = w3 * (picked[t][:, p * LANES:(p + 1) * LANES] + ones)
                    rest = prod - jnp.where(rest_lanes, prod.astype(BF16).astype(F32), 0.0)
                    rest = rest - jnp.where(low_lanes, rest.astype(BF16).astype(F32), 0.0)
                    w_scr[(g * PICKS + t) * 2 + p] = rest.astype(BF16)
            return unused

        lax.fori_loop(0, steps // (4 * PICKS), build, 0)
    else:
        mods_t = get_mods_t()
        w_scr[0] = (w3 * jnp.where(lane < chans, 2.0, 0.0)).astype(BF16)

    ones_rows = jnp.ones((chans, width), BF16)
    zero_rows = jnp.zeros((half_lanes, width), BF16)
    unroll = UNROLL if fold else 2 * AHEAD
    groups = tiles // unroll
    per_chunk = SWEEPS * groups
    early = max(unroll - EARLY, 0)

    def half_pre(t, x):
        tops = [jnp.concatenate([x[p], x[p], x[p], ones_rows], axis=0) for p in range(2)]
        if fold:
            left = jnp.concatenate([tops[0], zero_rows], axis=0)
            right = jnp.concatenate([zero_rows, tops[1]], axis=0)
            return jnp.dot(w_scr[t], jnp.concatenate([left, right], axis=1), preferred_element_type=F32)
        rhs = jnp.concatenate([jnp.concatenate([top, zero_rows], axis=0) for top in tops], axis=1)
        pre = jnp.dot(w_scr[0], rhs, preferred_element_type=F32)
        src = scale_row(2 * t + wide_lane // width, per)
        scale = jnp.dot(mods_t, one_hot(wide_row == src), preferred_element_type=F32)
        shift = jnp.dot(mods_t, one_hot(wide_row == src + per), preferred_element_type=F32)
        return 0.5 * (pre * (1.0 + scale) + shift)

    def project(hidden):
        return jnp.dot(w_out_t, hidden, preferred_element_type=F32)

    def load_xs(t):
        return xs_scr[2 * t], xs_scr[2 * t + 1]

    def advance(g, t, d, d_prev, total, first=None):
        c = jnp.maximum(g, 0) // per_chunk
        lanes = pl.ds(pl.multiple_of(lax.rem(c, cuts) * width, width), width)
        x0 = x_scr[c]
        x_next = x_scr[jnp.minimum((g + per_chunk) // per_chunk, chunks - 1)]
        last = lax.rem(g + per_chunk, per_chunk) >= per_chunk - groups
        for p in range(2):
            j = 2 * t + p
            i = jnp.maximum(j - 1, 0)
            part = d[:, p * width:(p + 1) * width]
            total = total + step_ref[i // per, 0, lax.rem(i, per)] * (0.5 * (d_prev + part))
            if p == 0 and first is not None:
                total = jnp.where(first, 0.0, total)
            new = x0 + total
            xs_scr[j] = jnp.where(last, x_next, new).astype(BF16)
            res_scr[j, c // cuts, :, lanes] = new
            d_prev = part
        return d_prev, total

    def send(b, cut=None):
        lanes = slice(None) if cut is None else pl.ds(cut * width, width)
        place = (slice(None), me * share + b, slice(None), lanes)
        for i in offsets(n):
            q = lax.rem(me + i, n)
            pltpu.make_async_remote_copy(
                res_scr.at[pl.ds(q * per, per), b, :, lanes], out_ref.at[place], send_sem, recv_sem,
                device_id={"time": q}, device_id_type=MESH).start()
        out_ref[place] = res_scr[pl.ds(me * per, per), b, :, lanes]

    def body(g, carry):
        t0 = lax.rem(g, groups) * unroll
        t_next = lax.rem(g + 1, groups) * unroll
        xs = [load_xs(t0 + u) for u in range(AHEAD, unroll)] + [load_xs(t_next + u) for u in range(AHEAD)]
        ds = [project(h_scr[...])]
        halves = {u: z_scr[u] for u in range(AHEAD)}
        for u in range(unroll):
            v = u + AHEAD
            if v < unroll:
                halves[v] = half_pre(t0 + v, xs[u])
            half = halves.pop(u)
            arg = half * (half * half * C3 + C1)
            hidden = (half * (1.0 + jnp.tanh(arg))).astype(BF16)
            if early <= u < early + AHEAD:
                z_scr[u - early] = half_pre(t_next + u - early, xs[u - early - AHEAD])
            if u < unroll - 1:
                ds.append(project(hidden))
            else:
                h_scr[...] = hidden
        carry = advance(g - 1, lax.rem(t0 + tiles - 1, tiles), ds[0], *carry)
        for u in range(unroll - 1):
            carry = advance(g, t0 + u, ds[u + 1], *carry, first=t0 == 0 if u == 0 else None)

        for c in range(cuts, chunks):
            if c % cuts == 0 or c > chunks - cuts:
                @pl.when(g == c * per_chunk)
                def _(c=c):
                    send((c - 1) // cuts, None if c % cuts == 0 else (c - 1) % cuts)

        return carry

    x_first = x_scr[0].astype(BF16)

    @pl.loop(0, steps)
    def _(j):
        xs_scr[j] = x_first

    for u in range(AHEAD):
        z_scr[u] = half_pre(u, (x_first, x_first))
    h_scr[...] = jnp.zeros_like(h_scr)
    zero = jnp.zeros((chans, width), F32)
    total_groups = chunks * per_chunk
    ready()
    carry = lax.fori_loop(0, total_groups, body, (zero, zero))
    advance(total_groups - 1, tiles - 1, project(h_scr[...]), *carry)
    send(share - 1, cuts - 1)
    wait_bytes(res_scr.at[pl.ds(0, (n - 1) * per)], recv_sem, send_sem)


def x_loads(me, x_hbm, x_scr, sem):
    chunks, _, width = x_scr.shape
    cuts = x_hbm.shape[2] // width
    return [
        pltpu.make_async_copy(
            x_hbm.at[me * (chunks // cuts) + c // cuts, :, pl.ds(c % cuts * width, width)], x_scr.at[c], sem.at[c])
        for c in range(chunks)
    ]


def folded_kernel(n, x_hbm, scale_hbm, shift_hbm, step_hbm, w_in_hbm, w_out_hbm, out_ref, mods_t_ref, steps_ref, flag_ref, scale, shift, step, w_in, w_out_t, mine, mine_step, mods, step_all, load_sem, x_sem, param_send, param_recv, x_scr, w_scr, xs_scr, z_scr, h_scr, res_scr, send_sem, recv_sem):
    me = lax.axis_index("time")
    per = scale.shape[0]
    loads = [
        pltpu.make_async_copy(src, dst, load_sem.at[k])
        for k, (src, dst) in enumerate((
            (scale_hbm, scale), (shift_hbm, shift), (step_hbm, step), (w_in_hbm, w_in), (w_out_hbm, w_out_t)))
    ] + x_loads(me, x_hbm, x_scr, x_sem)
    for load in loads:
        load.start()
    signal_all(n, me)
    for load in loads:
        load.wait()
    share_parameters(n, me, scale, shift, step, mine, mine_step, mods, steps_ref, param_send, param_recv)

    def get_mods_t():
        wait_bytes(mods.at[pl.ds(0, n - 1)], param_recv.at[0])
        parts = [mods[q].astype(F32) for q in range(n)]
        flag_ref[0] = fold_is_safe(parts, per, w_in[...])
        flat = jnp.concatenate(parts, axis=0).astype(BF16)
        r = lax.broadcasted_iota(jnp.int32, (LANES, LANES), 0)
        c = lax.broadcasted_iota(jnp.int32, (LANES, LANES), 1)
        mods_t = lax.dot_general(flat, one_hot(r == c), CONTRACT0, preferred_element_type=F32).astype(BF16)
        mods_t_ref[...] = mods_t
        return mods_t

    def ready():
        wait_bytes(steps_ref.at[pl.ds(0, n - 1)], param_recv.at[1], param_send.at[1])
        wait_bytes(mods.at[pl.ds(0, n - 1)], param_send.at[0])
        to_scalars = pltpu.make_async_copy(steps_ref, step_all, load_sem.at[0])
        to_scalars.start()
        to_scalars.wait()

    run_sweeps(n, per, True, me, get_mods_t, w_in[...], w_out_t[...], ready, step_all, out_ref, x_scr, w_scr, xs_scr, z_scr, h_scr, res_scr, send_sem, recv_sem)


def wide_kernel(n, per, x_hbm, mods_t_ref, w_in_ref, w_out_ref, step_ref, out_ref, x_sem, x_scr, w_scr, xs_scr, z_scr, h_scr, res_scr, send_sem, recv_sem):
    me = lax.axis_index("time")
    loads = x_loads(me, x_hbm, x_scr, x_sem)
    for load in loads:
        load.start()
    signal_all(n, me)
    for load in loads:
        load.wait()

    def ready():
        pl.semaphore_wait(pltpu.get_barrier_semaphore(), n - 1)

    run_sweeps(n, per, False, me, lambda: mods_t_ref[...], w_in_ref[...], w_out_ref[...], ready, step_ref, out_ref, x_scr, w_scr, xs_scr, z_scr, h_scr, res_scr, send_sem, recv_sem)


def solution(mesh):
    n = mesh.shape["time"]
    vmem = pl.BlockSpec(memory_space=pltpu.VMEM)
    smem = pl.BlockSpec(memory_space=pltpu.SMEM)

    def local(x_init, w_in, w_out, mod_scale, mod_shift, step_size):
        batch, tokens, chans = x_init.shape
        per, hidden = mod_scale.shape
        share = batch // n
        any_spec = pl.BlockSpec(memory_space=pl.ANY)
        steps = n * per
        chunks = share * tokens // WIDTH
        x_t = jnp.swapaxes(x_init, 1, 2)
        out_type = jax.ShapeDtypeStruct((per, batch, chans, tokens), F32)
        dma = pltpu.SemaphoreType.DMA

        def scratch(folded):
            return [
                pltpu.VMEM((chunks, chans, WIDTH), F32),
                pltpu.VMEM((steps // 2 if folded else 1, hidden, LANES), BF16),
                pltpu.VMEM((steps, chans, WIDTH), BF16),
                pltpu.VMEM((AHEAD, hidden, 2 * WIDTH), F32),
                pltpu.VMEM((hidden, 2 * WIDTH), BF16),
                pltpu.VMEM((steps, share, chans, tokens), F32),
                dma,
                dma,
            ]

        out, mods_t, step_all, flag = pl.pallas_call(
            functools.partial(folded_kernel, n),
            out_shape=(
                out_type,
                jax.ShapeDtypeStruct((hidden, LANES), BF16),
                jax.ShapeDtypeStruct((n, 1, LANES), F32),
                jax.ShapeDtypeStruct((1,), jnp.int32),
            ),
            in_specs=[any_spec] * 6,
            out_specs=(vmem, vmem, vmem, smem),
            scratch_shapes=[
                pltpu.VMEM((per, hidden), BF16),
                pltpu.VMEM((per, hidden), BF16),
                pltpu.SMEM((per,), F32),
                pltpu.VMEM((chans, hidden), BF16),
                pltpu.VMEM((chans, hidden), BF16),
                pltpu.VMEM((2 * per, hidden), BF16),
                pltpu.VMEM((1, LANES), F32),
                pltpu.VMEM((n, 2 * per, hidden), BF16),
                pltpu.SMEM((n, 1, LANES), F32),
                dma((5,)),
                dma((chunks,)),
                dma((2,)),
                dma((2,)),
            ] + scratch(True),
            compiler_params=pltpu.CompilerParams(collective_id=0, has_side_effects=True, vmem_limit_bytes=56 * 1024 * 1024),
            name="folded",
        )(x_t, mod_scale, mod_shift, step_size, w_in, w_out.T)

        def wide(out, mods_t, step_all):
            return pl.pallas_call(
                functools.partial(wide_kernel, n, per),
                out_shape=out_type,
                in_specs=[any_spec] + [vmem] * 3 + [smem],
                out_specs=vmem,
                scratch_shapes=[dma((chunks,))] + scratch(False),
                compiler_params=pltpu.CompilerParams(collective_id=1, has_side_effects=True, vmem_limit_bytes=40 * 1024 * 1024),
                name="wide",
            )(x_t, mods_t, w_in, w_out.T, step_all)

        out = lax.cond(flag[0] != 0, lambda out, *rest: out, wide, out, mods_t, step_all)
        return jnp.swapaxes(out, 2, 3)

    return jax.shard_map(local, mesh=mesh, in_specs=(P("data"), P(), P(), P("time"), P("time"), P("time")), out_specs=P("time", "data"), check_vma=False)
```

time: 87.9 us -> 86.1 us (0.980)
  Pallas kernels: 85.6 us -> 83.9 us
    pallas_call x2 -> x1, Pallas kernels: 85.6 us -> 83.9 us  [local(): pl.pallas_call(functools.partial(folded_kernel, n), out_shape=(out_type,...]
where the time goes in v5:
time: 86.1 us; the launch traced here: 85.9 us
  Pallas kernels  83.9 us (97%)
  local copies, waits for them, and re-layouts  1.32 us (2%)
    pallas_call x1, Pallas kernels, local(): pl.pallas_call(functools.partial(folded_kernel, n), out_shape=(out_type,...  83.9 us

profile of v5, /device:TPU:97, one launch (start us, length us, event | category | flops | bytes accessed | tf_op | source)
XLA Modules:
  0.0 85.9 jit_solution(11755444394638361876)
XLA Ops:
  0.0 83.9 %folded.1 = (f32[2,64,16,256]{3,2,1,0:T(8,128)S(1)}, bf16[384,128]{1,0:T(8,128)(2,1)S(1)}, f32[32,1,128]{2,1,0:T(1,128)S(1)}, s32[1]{0:T(128)}) custom-call(f32[64,16,256]{2,1,0:T(8,128)} %bitcast.5, bf16[2,384]{1,0:T(2,128)(2,1)} %scale_hbm.1, bf16[2,384]{1,0:T(2,128)(2,1)} %shift_hbm.1, f32[2]{0:T(128)} %step_hbm.1, bf16[16,384]{1,0:T(8,128)(2,1)} %w_in_hbm.1, ...), custom_call_target="tpu_custom_call" | custom-call | tf_op jit(solution)/shard_map/folded/pallas_call | solution.py:314
  84.6 1.3 %copy.10 = f32[2,64,256,16]{2,3,1,0:T(8,128)} copy(f32[2,64,256,16]{2,3,1,0:T(8,128)S(1)} %bitcast.7) | data formatting | bytes 4194304
  (1 shorter events, 0.0 us)

commit v6 on v5

--- a/solution.py
+++ b/solution.py
@@ -90,13 +90,12 @@
     wide_lane = lax.broadcasted_iota(jnp.int32, (1, 2 * LANES), 1)
 
     if fold:
+        fixed = jnp.where(slot < chans, w3, 0.0)
         w3 = w3 + jnp.where(slot == 3 * chans, 0.5, 0.0)
-        ones = jnp.where(slot < 3 * chans, 1.0, 0.0)
-        rest_lanes = (slot >= chans) & (slot < 3 * chans)
         low_lanes = (slot >= 2 * chans) & (slot < 3 * chans)
         wide_slot = lax.rem(wide_lane, half_lanes)
         source = scale_row(wide_lane // half_lanes, per) + jnp.where(wide_slot == 3 * chans, per, 0)
-        source = jnp.where(wide_slot <= 3 * chans, source, -8 * steps)
+        source = jnp.where((wide_slot >= chans) & (wide_slot <= 3 * chans), source, -8 * steps)
         ahead = wide_row - source
         mods_t = get_mods_t()
 
@@ -107,9 +106,8 @@
                 picked.append(jnp.dot(mods_t, one_hot(ahead == first), preferred_element_type=F32))
             for t in range(PICKS):
                 for p in range(2):
-                    prod = w3 * (picked[t][:, p * LANES:(p + 1) * LANES] + ones)
-                    rest = prod - jnp.where(rest_lanes, prod.astype(BF16).astype(F32), 0.0)
-                    rest = rest - jnp.where(low_lanes, rest.astype(BF16).astype(F32), 0.0)
+                    prod = w3 * picked[t][:, p * LANES:(p + 1) * LANES] + fixed
+                    rest = prod - jnp.where(low_lanes, prod.astype(BF16).astype(F32), 0.0)
                     w_scr[(g * PICKS + t) * 2 + p] = rest.astype(BF16)
             return unused
 
@@ -154,7 +152,7 @@
             j = 2 * t + p
             i = jnp.maximum(j - 1, 0)
             part = d[:, p * width:(p + 1) * width]
-            total = total + step_ref[i // per, 0, lax.rem(i, per)] * (0.5 * (d_prev + part))
+            total = total + (0.5 * step_ref[i // per, 0, lax.rem(i, per)]) * (d_prev + part)
             if p == 0 and first is not None:
                 total = jnp.where(first, 0.0, total)
             new = x0 + total

time: 86.1 us -> 85.1 us (0.988)
  Pallas kernels: 83.9 us -> 82.9 us
    pallas_call x1, Pallas kernels: 83.9 us -> 82.9 us  [local(): pl.pallas_call(functools.partial(folded_kernel, n), out_shape=(out_type,...]
where the time goes in v6:
time: 85.1 us; the launch traced here: 84.9 us
  Pallas kernels  82.9 us (97%)
  local copies, waits for them, and re-layouts  1.32 us (2%)
    pallas_call x1, Pallas kernels, local(): pl.pallas_call(functools.partial(folded_kernel, n), out_shape=(out_type,...  82.9 us

profile of v6, /device:TPU:97, one launch (start us, length us, event | category | flops | bytes accessed | tf_op | source)
XLA Modules:
  0.0 84.9 jit_solution(2730681164660022623)
XLA Ops:
  0.0 82.9 %folded.1 = (f32[2,64,16,256]{3,2,1,0:T(8,128)S(1)}, bf16[384,128]{1,0:T(8,128)(2,1)S(1)}, f32[32,1,128]{2,1,0:T(1,128)S(1)}, s32[1]{0:T(128)}) custom-call(f32[64,16,256]{2,1,0:T(8,128)} %bitcast.5, bf16[2,384]{1,0:T(2,128)(2,1)} %scale_hbm.1, bf16[2,384]{1,0:T(2,128)(2,1)} %shift_hbm.1, f32[2]{0:T(128)} %step_hbm.1, bf16[16,384]{1,0:T(8,128)(2,1)} %w_in_hbm.1, ...), custom_call_target="tpu_custom_call" | custom-call | tf_op jit(solution)/shard_map/folded/pallas_call | solution.py:312
  83.6 1.3 %copy.10 = f32[2,64,256,16]{2,3,1,0:T(8,128)} copy(f32[2,64,256,16]{2,3,1,0:T(8,128)S(1)} %bitcast.7) | data formatting | bytes 4194304
  (1 shorter events, 0.0 us)

commit v7 on v6

--- a/solution.py
+++ b/solution.py
@@ -10,7 +10,7 @@
 
 SWEEPS = 4
 UNROLL = 16
-PICKS = 4
+GROUPS = 4
 EARLY = 9
 AHEAD = 2
 LANES = 128
@@ -54,25 +54,30 @@
     mods[me] = mine[...]
     steps[me] = mine_step[...]
     pl.semaphore_wait(pltpu.get_barrier_semaphore(), n - 1)
-    for k, (src, dst) in enumerate(((mine, mods), (mine_step, steps))):
-        for i in offsets(n):
-            pltpu.make_async_remote_copy(
-                src, dst.at[me], send_sem.at[k], recv_sem.at[k],
-                device_id={"time": lax.rem(me + i, n)}, device_id_type=MESH).start()
-
-
-def fold_is_safe(parts, per, w_in):
-    top = 0.0
-    for part in parts:
-        top = jnp.maximum(top, jnp.abs(1.0 + part[:per]))
-    return (jnp.max(top) * jnp.max(jnp.abs(w_in.astype(F32))) <= FOLD_LIMIT).astype(jnp.int32)
+    size = n // GROUPS
+    for i in offsets(n):
+        q = lax.rem(me + i, n)
+        group = lax.rem(me // size - q // size + GROUPS, GROUPS)
+        pltpu.make_async_remote_copy(
+            mine, mods.at[me], send_sem.at[0], recv_sem.at[group], device_id={"time": q}, device_id_type=MESH).start()
+    for i in offsets(n):
+        pltpu.make_async_remote_copy(
+            mine_step, steps.at[me], send_sem.at[1], recv_sem.at[GROUPS],
+            device_id={"time": lax.rem(me + i, n)}, device_id_type=MESH).start()
+
+
+def transposed(parts):
+    rows = jnp.concatenate(parts, axis=0)
+    if rows.shape[0] < LANES:
+        rows = jnp.concatenate([rows, jnp.zeros((LANES - rows.shape[0], rows.shape[1]), F32)], axis=0)
+    return rows.T.astype(BF16)
 
 
 def scale_row(j, per):
     return j // per * (2 * per) + lax.rem(j, per)
 
 
-def run_sweeps(n, per, fold, me, get_mods_t, w_in, w_out_t, ready, step_ref, out_ref, x_scr, w_scr, xs_scr, z_scr, h_scr, res_scr, send_sem, recv_sem):
+def run_sweeps(n, per, fold, me, get_mods, w_in, w_out_t, ready, step_ref, out_ref, x_scr, w_scr, xs_scr, z_scr, h_scr, res_scr, send_sem, recv_sem):
     chunks, chans, width = x_scr.shape
     tokens = res_scr.shape[3]
     cuts = tokens // width
@@ -82,6 +87,13 @@
     half_lanes = LANES // 2
 
     row = lax.broadcasted_iota(jnp.int32, (LANES, LANES), 0)
+    x_first = x_scr[0].astype(BF16)
+
+    @pl.loop(0, steps)
+    def _(j):
+        xs_scr[j] = x_first
+
+    h_scr[...] = jnp.zeros_like(h_scr)
     lane = lax.broadcasted_iota(jnp.int32, (1, LANES), 1)
     slot = lax.rem(lane, half_lanes)
     spread = one_hot((lax.rem(lane, chans) == row) & (slot < 3 * chans))
@@ -96,24 +108,17 @@
         wide_slot = lax.rem(wide_lane, half_lanes)
         source = scale_row(wide_lane // half_lanes, per) + jnp.where(wide_slot == 3 * chans, per, 0)
         source = jnp.where((wide_slot >= chans) & (wide_slot <= 3 * chans), source, -8 * steps)
-        ahead = wide_row - source
-        mods_t = get_mods_t()
-
-        def build(g, unused):
-            picked = []
-            for t in range(PICKS):
-                first = (g * PICKS + t) * 8
-                picked.append(jnp.dot(mods_t, one_hot(ahead == first), preferred_element_type=F32))
-            for t in range(PICKS):
-                for p in range(2):
-                    prod = w3 * picked[t][:, p * LANES:(p + 1) * LANES] + fixed
-                    rest = prod - jnp.where(low_lanes, prod.astype(BF16).astype(F32), 0.0)
-                    w_scr[(g * PICKS + t) * 2 + p] = rest.astype(BF16)
-            return unused
-
-        lax.fori_loop(0, steps // (4 * PICKS), build, 0)
+        picks = [one_hot(wide_row - 8 * t == source) for t in range(n // GROUPS * per // 4)]
+        for k in range(GROUPS):
+            first, mods_t = get_mods(k)
+            picked = [jnp.dot(mods_t, pick, preferred_element_type=F32) for pick in picks]
+            for t in range(2 * len(picks)):
+                mod = picked[t // 2][:, t % 2 * LANES:(t % 2 + 1) * LANES]
+                prod = w3 * mod + fixed
+                rest = prod - jnp.where(low_lanes, prod.astype(BF16).astype(F32), 0.0)
+                w_scr[first * per // 2 + t] = rest.astype(BF16)
     else:
-        mods_t = get_mods_t()
+        mods_t = get_mods()
         w_scr[0] = (w3 * jnp.where(lane < chans, 2.0, 0.0)).astype(BF16)
 
     ones_rows = jnp.ones((chans, width), BF16)
@@ -202,15 +207,8 @@
 
         return carry
 
-    x_first = x_scr[0].astype(BF16)
-
-    @pl.loop(0, steps)
-    def _(j):
-        xs_scr[j] = x_first
-
     for u in range(AHEAD):
         z_scr[u] = half_pre(u, (x_first, x_first))
-    h_scr[...] = jnp.zeros_like(h_scr)
     zero = jnp.zeros((chans, width), F32)
     total_groups = chunks * per_chunk
     ready()
@@ -230,7 +228,7 @@
     ]
 
 
-def folded_kernel(n, x_hbm, scale_hbm, shift_hbm, step_hbm, w_in_hbm, w_out_hbm, out_ref, mods_t_ref, steps_ref, flag_ref, scale, shift, step, w_in, w_out_t, mine, mine_step, mods, step_all, load_sem, x_sem, param_send, param_recv, x_scr, w_scr, xs_scr, z_scr, h_scr, res_scr, send_sem, recv_sem):
+def folded_kernel(n, x_hbm, scale_hbm, shift_hbm, step_hbm, w_in_hbm, w_out_hbm, out_ref, mods, steps_ref, flag_ref, scale, shift, step, w_in, w_out_t, mine, mine_step, step_all, load_sem, x_sem, param_send, param_recv, x_scr, w_scr, xs_scr, z_scr, h_scr, res_scr, send_sem, recv_sem):
     me = lax.axis_index("time")
     per = scale.shape[0]
     loads = [
@@ -245,28 +243,29 @@
         load.wait()
     share_parameters(n, me, scale, shift, step, mine, mine_step, mods, steps_ref, param_send, param_recv)
 
-    def get_mods_t():
-        wait_bytes(mods.at[pl.ds(0, n - 1)], param_recv.at[0])
-        parts = [mods[q].astype(F32) for q in range(n)]
-        flag_ref[0] = fold_is_safe(parts, per, w_in[...])
-        flat = jnp.concatenate(parts, axis=0).astype(BF16)
-        r = lax.broadcasted_iota(jnp.int32, (LANES, LANES), 0)
-        c = lax.broadcasted_iota(jnp.int32, (LANES, LANES), 1)
-        mods_t = lax.dot_general(flat, one_hot(r == c), CONTRACT0, preferred_element_type=F32).astype(BF16)
-        mods_t_ref[...] = mods_t
-        return mods_t
+    tops = []
+
+    def get_mods(k):
+        size = n // GROUPS
+        wait_bytes(mods.at[pl.ds(0, size if k else size - 1)], param_recv.at[k])
+        first = lax.rem(me // size + k, GROUPS) * size
+        parts = [mods[first + q].astype(F32) for q in range(size)]
+        tops.extend(jnp.abs(1.0 + part[:per]) for part in parts)
+        return first, transposed(parts)
 
     def ready():
-        wait_bytes(steps_ref.at[pl.ds(0, n - 1)], param_recv.at[1], param_send.at[1])
+        top = functools.reduce(jnp.maximum, tops)
+        flag_ref[0] = (jnp.max(top) * jnp.max(jnp.abs(w_in[...].astype(F32))) <= FOLD_LIMIT).astype(jnp.int32)
+        wait_bytes(steps_ref.at[pl.ds(0, n - 1)], param_recv.at[GROUPS], param_send.at[1])
         wait_bytes(mods.at[pl.ds(0, n - 1)], param_send.at[0])
         to_scalars = pltpu.make_async_copy(steps_ref, step_all, load_sem.at[0])
         to_scalars.start()
         to_scalars.wait()
 
-    run_sweeps(n, per, True, me, get_mods_t, w_in[...], w_out_t[...], ready, step_all, out_ref, x_scr, w_scr, xs_scr, z_scr, h_scr, res_scr, send_sem, recv_sem)
-
-
-def wide_kernel(n, per, x_hbm, mods_t_ref, w_in_ref, w_out_ref, step_ref, out_ref, x_sem, x_scr, w_scr, xs_scr, z_scr, h_scr, res_scr, send_sem, recv_sem):
+    run_sweeps(n, per, True, me, get_mods, w_in[...], w_out_t[...], ready, step_all, out_ref, x_scr, w_scr, xs_scr, z_scr, h_scr, res_scr, send_sem, recv_sem)
+
+
+def wide_kernel(n, per, x_hbm, mods, w_in_ref, w_out_ref, step_ref, out_ref, x_sem, x_scr, w_scr, xs_scr, z_scr, h_scr, res_scr, send_sem, recv_sem):
     me = lax.axis_index("time")
     loads = x_loads(me, x_hbm, x_scr, x_sem)
     for load in loads:
@@ -278,7 +277,7 @@
     def ready():
         pl.semaphore_wait(pltpu.get_barrier_semaphore(), n - 1)
 
-    run_sweeps(n, per, False, me, lambda: mods_t_ref[...], w_in_ref[...], w_out_ref[...], ready, step_ref, out_ref, x_scr, w_scr, xs_scr, z_scr, h_scr, res_scr, send_sem, recv_sem)
+    run_sweeps(n, per, False, me, lambda: transposed([mods[q].astype(F32) for q in range(n)]), w_in_ref[...], w_out_ref[...], ready, step_ref, out_ref, x_scr, w_scr, xs_scr, z_scr, h_scr, res_scr, send_sem, recv_sem)
 
 
 def solution(mesh):
@@ -309,11 +308,11 @@
                 dma,
             ]
 
-        out, mods_t, step_all, flag = pl.pallas_call(
+        out, mods, step_all, flag = pl.pallas_call(
             functools.partial(folded_kernel, n),
             out_shape=(
                 out_type,
-                jax.ShapeDtypeStruct((hidden, LANES), BF16),
+                jax.ShapeDtypeStruct((n, 2 * per, hidden), BF16),
                 jax.ShapeDtypeStruct((n, 1, LANES), F32),
                 jax.ShapeDtypeStruct((1,), jnp.int32),
             ),
@@ -327,18 +326,17 @@
                 pltpu.VMEM((chans, hidden), BF16),
                 pltpu.VMEM((2 * per, hidden), BF16),
                 pltpu.VMEM((1, LANES), F32),
-                pltpu.VMEM((n, 2 * per, hidden), BF16),
                 pltpu.SMEM((n, 1, LANES), F32),
                 dma((5,)),
                 dma((chunks,)),
                 dma((2,)),
-                dma((2,)),
+                dma((GROUPS + 1,)),
             ] + scratch(True),
             compiler_params=pltpu.CompilerParams(collective_id=0, has_side_effects=True, vmem_limit_bytes=56 * 1024 * 1024),
             name="folded",
         )(x_t, mod_scale, mod_shift, step_size, w_in, w_out.T)
 
-        def wide(out, mods_t, step_all):
+        def wide(out, mods, step_all):
             return pl.pallas_call(
                 functools.partial(wide_kernel, n, per),
                 out_shape=out_type,
@@ -347,9 +345,9 @@
                 scratch_shapes=[dma((chunks,))] + scratch(False),
                 compiler_params=pltpu.CompilerParams(collective_id=1, has_side_effects=True, vmem_limit_bytes=40 * 1024 * 1024),
                 name="wide",
-            )(x_t, mods_t, w_in, w_out.T, step_all)
-
-        out = lax.cond(flag[0] != 0, lambda out, *rest: out, wide, out, mods_t, step_all)
+            )(x_t, mods, w_in, w_out.T, step_all)
+
+        out = lax.cond(flag[0] != 0, lambda out, *rest: out, wide, out, mods, step_all)
         return jnp.swapaxes(out, 2, 3)
 
     return jax.shard_map(local, mesh=mesh, in_specs=(P("data"), P(), P(), P("time"), P("time"), P("time")), out_specs=P("time", "data"), check_vma=False)

time: 85.1 us -> 83.8 us (0.985)
  Pallas kernels: 82.9 us -> 81.6 us
    pallas_call x1, Pallas kernels: 82.9 us -> 81.6 us  [local(): pl.pallas_call(functools.partial(folded_kernel, n), out_shape=(out_type,...]
where the time goes in v7:
time: 83.8 us; the launch traced here: 83.6 us
  Pallas kernels  81.6 us (97%)
  local copies, waits for them, and re-layouts  1.32 us (2%)
    pallas_call x1, Pallas kernels, local(): pl.pallas_call(functools.partial(folded_kernel, n), out_shape=(out_type,...  81.6 us

profile of v7, /device:TPU:97, one launch (start us, length us, event | category | flops | bytes accessed | tf_op | source)
XLA Modules:
  0.0 83.6 jit_solution(1657437721410524311)
XLA Ops:
  0.0 81.6 %folded.1 = (f32[2,64,16,256]{3,2,1,0:T(8,128)S(1)}, bf16[32,4,384]{2,1,0:T(4,128)(2,1)S(1)}, f32[32,1,128]{2,1,0:T(1,128)S(1)}, s32[1]{0:T(128)}) custom-call(f32[64,16,256]{2,1,0:T(8,128)} %bitcast.5, bf16[2,384]{1,0:T(2,128)(2,1)} %scale_hbm.1, bf16[2,384]{1,0:T(2,128)(2,1)} %shift_hbm.1, f32[2]{0:T(128)} %step_hbm.1, bf16[16,384]{1,0:T(8,128)(2,1)} %w_in_hbm.1, ...), custom_call_target="tpu_custom_call" | custom-call | tf_op jit(solution)/shard_map/folded/pallas_call | solution.py:311
  82.3 1.3 %copy.10 = f32[2,64,256,16]{2,3,1,0:T(8,128)} copy(f32[2,64,256,16]{2,3,1,0:T(8,128)S(1)} %bitcast.7) | data formatting | bytes 4194304
  (1 shorter events, 0.0 us)

commit v8 on v7

--- a/solution.py
+++ b/solution.py
@@ -11,7 +11,7 @@
 SWEEPS = 4
 UNROLL = 16
 GROUPS = 4
-EARLY = 9
+EARLY = 5
 AHEAD = 2
 LANES = 128
 WIDTH = 128
@@ -159,10 +159,9 @@
             part = d[:, p * width:(p + 1) * width]
             total = total + (0.5 * step_ref[i // per, 0, lax.rem(i, per)]) * (d_prev + part)
             if p == 0 and first is not None:
-                total = jnp.where(first, 0.0, total)
-            new = x0 + total
-            xs_scr[j] = jnp.where(last, x_next, new).astype(BF16)
-            res_scr[j, c // cuts, :, lanes] = new
+                total = jnp.where(first, x0, total)
+            xs_scr[j] = jnp.where(last, x_next, total).astype(BF16)
+            res_scr[j, c // cuts, :, lanes] = total
             d_prev = part
         return d_prev, total
 
@@ -212,7 +211,7 @@
     zero = jnp.zeros((chans, width), F32)
     total_groups = chunks * per_chunk
     ready()
-    carry = lax.fori_loop(0, total_groups, body, (zero, zero))
+    carry = lax.fori_loop(0, total_groups, body, (zero, x_scr[0]))
     advance(total_groups - 1, tiles - 1, project(h_scr[...]), *carry)
     send(share - 1, cuts - 1)
     wait_bytes(res_scr.at[pl.ds(0, (n - 1) * per)], recv_sem, send_sem)

time: 83.8 us -> 83.2 us (level)
  no operation moved by 1% of the time
where the time goes in v8:
time: 83.2 us; the launch traced here: 83.1 us
  Pallas kernels  81.1 us (97%)
  local copies, waits for them, and re-layouts  1.32 us (2%)
    pallas_call x1, Pallas kernels, local(): pl.pallas_call(functools.partial(folded_kernel, n), out_shape=(out_type,...  81.1 us

profile of v8, /device:TPU:97, one launch (start us, length us, event | category | flops | bytes accessed | tf_op | source)
XLA Modules:
  0.0 83.1 jit_solution(14464118529716970604)
XLA Ops:
  0.0 81.1 %folded.1 = (f32[2,64,16,256]{3,2,1,0:T(8,128)S(1)}, bf16[32,4,384]{2,1,0:T(4,128)(2,1)S(1)}, f32[32,1,128]{2,1,0:T(1,128)S(1)}, s32[1]{0:T(128)}) custom-call(f32[64,16,256]{2,1,0:T(8,128)} %bitcast.5, bf16[2,384]{1,0:T(2,128)(2,1)} %scale_hbm.1, bf16[2,384]{1,0:T(2,128)(2,1)} %shift_hbm.1, f32[2]{0:T(128)} %step_hbm.1, bf16[16,384]{1,0:T(8,128)(2,1)} %w_in_hbm.1, ...), custom_call_target="tpu_custom_call" | custom-call | tf_op jit(solution)/shard_map/folded/pallas_call | solution.py:310
  81.8 1.3 %copy.10 = f32[2,64,256,16]{2,3,1,0:T(8,128)} copy(f32[2,64,256,16]{2,3,1,0:T(8,128)S(1)} %bitcast.7) | data formatting | bytes 4194304
  (1 shorter events, 0.0 us)

commit v9 on v8

--- a/solution.py
+++ b/solution.py
@@ -109,7 +109,7 @@
         source = scale_row(wide_lane // half_lanes, per) + jnp.where(wide_slot == 3 * chans, per, 0)
         source = jnp.where((wide_slot >= chans) & (wide_slot <= 3 * chans), source, -8 * steps)
         picks = [one_hot(wide_row - 8 * t == source) for t in range(n // GROUPS * per // 4)]
-        for k in range(GROUPS):
+        for k in sorted(range(GROUPS), key=lambda k: min(k, GROUPS - k)):
             first, mods_t = get_mods(k)
             picked = [jnp.dot(mods_t, pick, preferred_element_type=F32) for pick in picks]
             for t in range(2 * len(picks)):
@@ -227,7 +227,7 @@
     ]
 
 
-def folded_kernel(n, x_hbm, scale_hbm, shift_hbm, step_hbm, w_in_hbm, w_out_hbm, out_ref, mods, steps_ref, flag_ref, scale, shift, step, w_in, w_out_t, mine, mine_step, step_all, load_sem, x_sem, param_send, param_recv, x_scr, w_scr, xs_scr, z_scr, h_scr, res_scr, send_sem, recv_sem):
+def folded_kernel(n, x_hbm, scale_hbm, shift_hbm, step_hbm, w_in_hbm, w_out_hbm, out_ref, mods, steps_ref, flag_hbm, scale, shift, step, w_in, w_out_t, mine, mine_step, step_all, flag, load_sem, x_sem, param_send, param_recv, x_scr, w_scr, xs_scr, z_scr, h_scr, res_scr, send_sem, recv_sem):
     me = lax.axis_index("time")
     per = scale.shape[0]
     loads = [
@@ -243,6 +243,7 @@
     share_parameters(n, me, scale, shift, step, mine, mine_step, mods, steps_ref, param_send, param_recv)
 
     tops = []
+    flag_copy = pltpu.make_async_copy(flag, flag_hbm, load_sem.at[1])
 
     def get_mods(k):
         size = n // GROUPS
@@ -254,7 +255,8 @@
 
     def ready():
         top = functools.reduce(jnp.maximum, tops)
-        flag_ref[0] = (jnp.max(top) * jnp.max(jnp.abs(w_in[...].astype(F32))) <= FOLD_LIMIT).astype(jnp.int32)
+        flag[0] = (jnp.max(top) * jnp.max(jnp.abs(w_in[...].astype(F32))) <= FOLD_LIMIT).astype(jnp.int32)
+        flag_copy.start()
         wait_bytes(steps_ref.at[pl.ds(0, n - 1)], param_recv.at[GROUPS], param_send.at[1])
         wait_bytes(mods.at[pl.ds(0, n - 1)], param_send.at[0])
         to_scalars = pltpu.make_async_copy(steps_ref, step_all, load_sem.at[0])
@@ -262,6 +264,7 @@
         to_scalars.wait()
 
     run_sweeps(n, per, True, me, get_mods, w_in[...], w_out_t[...], ready, step_all, out_ref, x_scr, w_scr, xs_scr, z_scr, h_scr, res_scr, send_sem, recv_sem)
+    flag_copy.wait()
 
 
 def wide_kernel(n, per, x_hbm, mods, w_in_ref, w_out_ref, step_ref, out_ref, x_sem, x_scr, w_scr, xs_scr, z_scr, h_scr, res_scr, send_sem, recv_sem):
@@ -316,7 +319,7 @@
                 jax.ShapeDtypeStruct((1,), jnp.int32),
             ),
             in_specs=[any_spec] * 6,
-            out_specs=(vmem, vmem, vmem, smem),
+            out_specs=(vmem, vmem, vmem, any_spec),
             scratch_shapes=[
                 pltpu.VMEM((per, hidden), BF16),
                 pltpu.VMEM((per, hidden), BF16),
@@ -326,6 +329,7 @@
                 pltpu.VMEM((2 * per, hidden), BF16),
                 pltpu.VMEM((1, LANES), F32),
                 pltpu.SMEM((n, 1, LANES), F32),
+                pltpu.SMEM((1,), jnp.int32),
                 dma((5,)),
                 dma((chunks,)),
                 dma((2,)),

time: 83.2 us -> 82.7 us (level)
  no operation moved by 1% of the time
where the time goes in v9:
time: 82.7 us; the launch traced here: 82.6 us
  Pallas kernels  80.6 us (97%)
  local copies, waits for them, and re-layouts  1.32 us (2%)
    pallas_call x1, Pallas kernels, local(): pl.pallas_call(functools.partial(folded_kernel, n), out_shape=(out_type,...  80.6 us

profile of v9, /device:TPU:97, one launch (start us, length us, event | category | flops | bytes accessed | tf_op | source)
XLA Modules:
  0.0 82.6 jit_solution(8513036621729274488)
XLA Ops:
  0.0 80.6 %folded.1 = (f32[2,64,16,256]{3,2,1,0:T(8,128)S(1)}, bf16[32,4,384]{2,1,0:T(4,128)(2,1)S(1)}, f32[32,1,128]{2,1,0:T(1,128)S(1)}, s32[1]{0:T(128)}) custom-call(f32[64,16,256]{2,1,0:T(8,128)} %bitcast.5, bf16[2,384]{1,0:T(2,128)(2,1)} %scale_hbm.1, bf16[2,384]{1,0:T(2,128)(2,1)} %shift_hbm.1, f32[2]{0:T(128)} %step_hbm.1, bf16[16,384]{1,0:T(8,128)(2,1)} %w_in_hbm.1, ...), custom_call_target="tpu_custom_call" | custom-call | tf_op jit(solution)/shard_map/folded/pallas_call | solution.py:313
  81.2 1.3 %copy.10 = f32[2,64,256,16]{2,3,1,0:T(8,128)} copy(f32[2,64,256,16]{2,3,1,0:T(8,128)S(1)} %bitcast.7) | data formatting | bytes 4194304
  (1 shorter events, 0.0 us)

commit v10 on v9

--- a/solution.py
+++ b/solution.py
@@ -46,11 +46,8 @@
     per = scale.shape[0]
     mine[0:per] = scale[...]
     mine[per:2 * per] = shift[...]
-    lane = lax.broadcasted_iota(jnp.int32, (1, LANES), 1)
-    row = jnp.zeros((1, LANES), F32)
     for i in range(per):
-        row = jnp.where(lane == i, step[i], row)
-    mine_step[...] = row
+        mine_step[i:i + 1] = jnp.full((1, LANES), 0.5 * step[i], F32)
     mods[me] = mine[...]
     steps[me] = mine_step[...]
     pl.semaphore_wait(pltpu.get_barrier_semaphore(), n - 1)
@@ -157,7 +154,7 @@
             j = 2 * t + p
             i = jnp.maximum(j - 1, 0)
             part = d[:, p * width:(p + 1) * width]
-            total = total + (0.5 * step_ref[i // per, 0, lax.rem(i, per)]) * (d_prev + part)
+            total = total + step_ref[i // per, pl.ds(lax.rem(i, per), 1)] * (d_prev + part)
             if p == 0 and first is not None:
                 total = jnp.where(first, x0, total)
             xs_scr[j] = jnp.where(last, x_next, total).astype(BF16)
@@ -227,7 +224,7 @@
     ]
 
 
-def folded_kernel(n, x_hbm, scale_hbm, shift_hbm, step_hbm, w_in_hbm, w_out_hbm, out_ref, mods, steps_ref, flag_hbm, scale, shift, step, w_in, w_out_t, mine, mine_step, step_all, flag, load_sem, x_sem, param_send, param_recv, x_scr, w_scr, xs_scr, z_scr, h_scr, res_scr, send_sem, recv_sem):
+def folded_kernel(n, x_hbm, scale_hbm, shift_hbm, step_hbm, w_in_hbm, w_out_hbm, out_ref, mods, steps_ref, flag_hbm, scale, shift, step, w_in, w_out_t, mine, mine_step, flag, load_sem, x_sem, param_send, param_recv, x_scr, w_scr, xs_scr, z_scr, h_scr, res_scr, send_sem, recv_sem):
     me = lax.axis_index("time")
     per = scale.shape[0]
     loads = [
@@ -259,11 +256,8 @@
         flag_copy.start()
         wait_bytes(steps_ref.at[pl.ds(0, n - 1)], param_recv.at[GROUPS], param_send.at[1])
         wait_bytes(mods.at[pl.ds(0, n - 1)], param_send.at[0])
-        to_scalars = pltpu.make_async_copy(steps_ref, step_all, load_sem.at[0])
-        to_scalars.start()
-        to_scalars.wait()
-
-    run_sweeps(n, per, True, me, get_mods, w_in[...], w_out_t[...], ready, step_all, out_ref, x_scr, w_scr, xs_scr, z_scr, h_scr, res_scr, send_sem, recv_sem)
+
+    run_sweeps(n, per, True, me, get_mods, w_in[...], w_out_t[...], ready, steps_ref, out_ref, x_scr, w_scr, xs_scr, z_scr, h_scr, res_scr, send_sem, recv_sem)
     flag_copy.wait()
 
 
@@ -285,7 +279,6 @@
 def solution(mesh):
     n = mesh.shape["time"]
     vmem = pl.BlockSpec(memory_space=pltpu.VMEM)
-    smem = pl.BlockSpec(memory_space=pltpu.SMEM)
 
     def local(x_init, w_in, w_out, mod_scale, mod_shift, step_size):
         batch, tokens, chans = x_init.shape
@@ -315,7 +308,7 @@
             out_shape=(
                 out_type,
                 jax.ShapeDtypeStruct((n, 2 * per, hidden), BF16),
-                jax.ShapeDtypeStruct((n, 1, LANES), F32),
+                jax.ShapeDtypeStruct((n, per, LANES), F32),
                 jax.ShapeDtypeStruct((1,), jnp.int32),
             ),
             in_specs=[any_spec] * 6,
@@ -327,8 +320,7 @@
                 pltpu.VMEM((chans, hidden), BF16),
                 pltpu.VMEM((chans, hidden), BF16),
                 pltpu.VMEM((2 * per, hidden), BF16),
-                pltpu.VMEM((1, LANES), F32),
-                pltpu.SMEM((n, 1, LANES), F32),
+                pltpu.VMEM((per, LANES), F32),
                 pltpu.SMEM((1,), jnp.int32),
                 dma((5,)),
                 dma((chunks,)),
@@ -343,7 +335,7 @@
             return pl.pallas_call(
                 functools.partial(wide_kernel, n, per),
                 out_shape=out_type,
-                in_specs=[any_spec] + [vmem] * 3 + [smem],
+                in_specs=[any_spec] + [vmem] * 4,
                 out_specs=vmem,
                 scratch_shapes=[dma((chunks,))] + scratch(False),
                 compiler_params=pltpu.CompilerParams(collective_id=1, has_side_effects=True, vmem_limit_bytes=40 * 1024 * 1024),

time: 82.7 us -> 81.8 us (0.989)
  Pallas kernels: 80.6 us -> 79.7 us
    pallas_call x1, Pallas kernels: 80.6 us -> 79.7 us  [local(): pl.pallas_call(functools.partial(folded_kernel, n), out_shape=(out_type,...]
where the time goes in v10:
time: 81.8 us; the launch traced here: 81.7 us
  Pallas kernels  79.7 us (97%)
  local copies, waits for them, and re-layouts  1.32 us (2%)
    pallas_call x1, Pallas kernels, local(): pl.pallas_call(functools.partial(folded_kernel, n), out_shape=(out_type,...  79.7 us

profile of v10, /device:TPU:97, one launch (start us, length us, event | category | flops | bytes accessed | tf_op | source)
XLA Modules:
  0.0 81.7 jit_solution(9003432386112522447)
XLA Ops:
  0.0 79.7 %folded.1 = (f32[2,64,16,256]{3,2,1,0:T(8,128)S(1)}, bf16[32,4,384]{2,1,0:T(4,128)(2,1)S(1)}, f32[32,2,128]{2,1,0:T(2,128)S(1)}, s32[1]{0:T(128)}) custom-call(f32[64,16,256]{2,1,0:T(8,128)} %bitcast.5, bf16[2,384]{1,0:T(2,128)(2,1)} %scale_hbm.1, bf16[2,384]{1,0:T(2,128)(2,1)} %shift_hbm.1, f32[2]{0:T(128)} %step_hbm.1, bf16[16,384]{1,0:T(8,128)(2,1)} %w_in_hbm.1, ...), custom_call_target="tpu_custom_call" | custom-call | tf_op jit(solution)/shard_map/folded/pallas_call | solution.py:306
  80.3 1.3 %copy.10 = f32[2,64,256,16]{2,3,1,0:T(8,128)} copy(f32[2,64,256,16]{2,3,1,0:T(8,128)S(1)} %bitcast.7) | data formatting | bytes 4194304
  (1 shorter events, 0.0 us)
